TPU v7x, 128 devices: a whole 4x4x4 slice. The times are simulated.
128 devices in a mesh: sub: 8 (over x, core), lat: 8 (over y_lo, z), lon: 2 (over y_hi).
Axes of the slice: x: 4, y: 4 (y_hi: 2, y_lo: 2; y = y_hi * 2 + y_lo), z: 4, core: 2. Of those that a mesh axis runs over, the one named last changes fastest.
Arguments:
- increment: float32 [8, 128, 128, 512], P('sub', 'lat', 'lon'), may hold values from -6 to 6
- multiplier: float32 [8, 128, 128, 512], P('sub', 'lat', 'lon'), may hold values from -6 to 6
- background: bfloat16 [8, 128, 128, 512], P('sub', 'lat', 'lon'), may hold values from -6 to 6
- obs_cotangent: bfloat16 [8, 16, 2048, 512], P('sub', ('lat', 'lon')), may hold values from -6 to 6
- obs_column: int32 [8, 16, 2048], P('sub', ('lat', 'lon')), may hold values from 0 to 1023
- obs_count: int32 [8, 16], P('sub'), may hold values from 1 to 2048, 16384 in all within a row
- transport: float32 [8, 512], replicated, may hold values from 0.015 to 0.1
- hidden_weight: bfloat16 [512, 1024], replicated, may hold values from -0.25 to 0.25
- hidden_bias: float32 [1024], replicated, may hold values from -3 to 3
- output_weight: bfloat16 [1024, 512], replicated, may hold values from -0.1875 to 0.1875
Outputs:
- model_error: float32 [8, 128, 128, 512], P('sub', 'lat', 'lon')
- gradient: float32 [8, 128, 128, 512], P('sub', 'lat', 'lon')
- obs_tangent: bfloat16 [8, 16, 2048, 512], P('sub', ('lat', 'lon'))
Inputs may be any that keep to these rules, and one draw needn't show every extreme that they name: `obs_count`: the counts of one subwindow sum to 16384, and one of them equals 2048. `obs_column`: slots at or beyond their block's count are unused.
All inputs are finite; a program needn't handle non-finite values.
Results may differ from a plain program's by a relative error of at most 0.0058.
Values may be sent and summed in bfloat16 or wider, within the bound.
No kernel may reach another device: no remote copies, remote signals or barrier semaphores. Data moves between devices by JAX's collectives and lax.ppermute only.
A program may use at most 128 MiB of HBM per device.

v0:
```python
import functools

import jax
import jax.numpy as jnp
from jax import lax
from jax.experimental import pallas as pl
from jax.experimental.pallas import tpu as pltpu
from jax.sharding import PartitionSpec as P


STEPS = 4
REACH = 2 * STEPS
EDGE = REACH - 2
LANES = 128
COLS_TILE = 256
SLOTS_TILE = 512
MIRROR = (3, 2, 1, 0, 7, 6, 5, 4)
TOKEN = jax.ShapeDtypeStruct((8, LANES), jnp.float32)


CHUNK = 4


def pack_kernel(inc, mul, low, high, strip, held, sems):
    lon = lax.axis_index("lon")
    rows, across = inc.shape[0], inc.shape[1]
    side = pl.multiple_of((across - REACH) * (1 - lon), REACH)
    copies = {}
    for start in range(0, rows, CHUNK):
        for f, src in enumerate((inc, mul)):
            part = pl.ds(start, CHUNK)
            copies[f, start] = pltpu.make_async_copy(src.at[part], held.at[f, part], sems.at[f, start // CHUNK])
            copies[f, start].start()
    for start in range(0, rows, CHUNK):
        for f in range(2):
            copies[f, start].wait()
            for r in range(start, start + CHUNK):
                row = held[f, r].astype(jnp.bfloat16)
                if r < REACH:
                    low[f, r] = row
                if r >= rows - REACH:
                    high[f, r - rows + REACH] = row
                strip[f, r] = held[f, r, pl.ds(side, REACH), :].astype(jnp.bfloat16)


def pack(increment, multiplier):
    rows, across, levels = increment.shape
    shapes = [(2, REACH, across), (2, REACH, across), (2, rows, REACH)]
    return pl.pallas_call(
        pack_kernel,
        in_specs=[pl.BlockSpec(memory_space=pltpu.HBM)] * 2,
        out_specs=[pl.BlockSpec(memory_space=pltpu.VMEM)] * 3,
        out_shape=[jax.ShapeDtypeStruct(s + (levels,), jnp.bfloat16) for s in shapes],
        scratch_shapes=[
            pltpu.VMEM((2,) + increment.shape, jnp.float32),
            pltpu.SemaphoreType.DMA((2, rows // CHUNK)),
        ],
        name="pack",
    )(increment, multiplier)


def corner_kernel(strip, _, low, high, token):
    rows = strip.shape[1]
    low[...] = strip[:, :EDGE]
    high[...] = strip[:, rows - EDGE :]
    token[...] = jnp.zeros_like(token)


def corners(strip, token):
    fields, _, wide, levels = strip.shape
    return pl.pallas_call(
        corner_kernel,
        out_shape=[jax.ShapeDtypeStruct((fields, EDGE, wide, levels), jnp.bfloat16)] * 2 + [TOKEN],
        compiler_params=pltpu.CompilerParams(vmem_limit_bytes=8 << 20),
        name="corners",
    )(strip, token)


def sweep(src, dst, taps, first, last, blocks):
    c0, c1, c2, c3, c4, c5, c6, c7 = taps
    group = 4

    def rows_of(it, carry):
        i = first + it * group
        for b in range(blocks):
            j = 8 + 8 * b
            at = [src[i - 2 + r, j : j + 8, :] for r in range(group + 4)]
            for r in range(group):
                total = at[r + 2] + c0 * at[r]
                total = total + c1 * at[r + 1]
                total = total + c2 * at[r + 3]
                total = total + c3 * at[r + 4]
                total = total + c4 * src[i + r, j - 2 : j + 6, :]
                total = total + c5 * src[i + r, j - 1 : j + 7, :]
                total = total + c6 * src[i + r, j + 1 : j + 9, :]
                total = total + c7 * src[i + r, j + 2 : j + 10, :]
                dst[i + r, j : j + 8, :] = total
        return carry

    lax.fori_loop(0, (last - first) // group, rows_of, 0)


def transport_kernel(
    crossing, inc, mul, above, below, strip, above_corner, below_corner, rates, _, out, token, bufs, other, sems
):
    lat, lon = lax.axis_index("lat"), lax.axis_index("lon")
    odd = lax.rem(lax.axis_index("sub"), 2)
    n_lat = lax.axis_size("lat")
    rows, across, levels = inc.shape
    tall = rows + 2 * REACH
    blocks = (across + REACH) // 8
    tiles = levels // LANES
    own = pl.multiple_of(8 + REACH * lon, 8)
    beside = pl.multiple_of(8 + across * (1 - lon), 8)
    f = 1 - odd if crossing else odd
    forward = f == 0

    def arriving(src, t):
        there = bufs.at[t, pl.ds(REACH, rows), pl.ds(own, across), :]
        return pltpu.make_async_copy(src.at[:, :, pl.ds(t * LANES, LANES)], there, sems.at[t])

    @pl.when(forward)
    def _():
        for t in range(tiles):
            arriving(inc, t).start()

    @pl.when(jnp.logical_not(forward))
    def _():
        for t in range(tiles):
            arriving(mul, t).start()

    token[...] = jnp.zeros_like(token)
    blank = jnp.zeros((8, LANES), jnp.float32)
    for r in range(tall):
        other[r] = jnp.zeros(other.shape[1:], jnp.float32)
        for t in range(tiles):
            bufs[t, r, 0:8, :] = blank
            bufs[t, r, 8 * blocks + 8 : 8 * blocks + 16, :] = blank
    for t in range(tiles):
        for r in (0, 1, tall - 2, tall - 1):
            bufs[t, r, pl.ds(beside, REACH), :] = blank
        for r in range(REACH):
            lanes = slice(t * LANES, (t + 1) * LANES)
            bufs[t, r, pl.ds(own, across), :] = above[f, r, :, lanes].astype(jnp.float32)
            bufs[t, rows + REACH + r, pl.ds(own, across), :] = below[f, r, :, lanes].astype(jnp.float32)
        for r in range(rows):
            bufs[t, REACH + r, pl.ds(beside, REACH), :] = strip[f, r, :, lanes].astype(jnp.float32)
        for r in range(EDGE):
            bufs[t, REACH - EDGE + r, pl.ds(beside, REACH), :] = above_corner[f, r, :, lanes].astype(jnp.float32)
            bufs[t, rows + REACH + r, pl.ds(beside, REACH), :] = below_corner[f, r, :, lanes].astype(jnp.float32)

    def tile_of(t, carry):
        lanes = pl.ds(pl.multiple_of(t * LANES, LANES), LANES)
        pltpu.make_async_copy(
            inc.at[:, :, lanes], bufs.at[t, pl.ds(REACH, rows), pl.ds(own, across), :], sems.at[t]
        ).wait()
        spread = [
            jnp.broadcast_to(jnp.where(forward, rates[k : k + 1, lanes], rates[m : m + 1, lanes]), (8, LANES))
            for k, m in enumerate(MIRROR)
        ]
        rest = spread[0]
        for k in range(1, 8):
            rest = rest + spread[k]
        center = 1.0 - rest
        taps = [c / center for c in spread]
        scale = (center * center) * (center * center)
        a, b = bufs.at[t], other
        for step in range(STEPS):
            first, last = 2 * (step + 1), tall - 2 * (step + 1)
            sweep(a, b, taps, first, last, blocks)
            if step < STEPS - 1:

                @pl.when(lat == 0)
                def _(b=b, first=first):
                    for r in range(first, REACH):
                        b[r] = jnp.zeros(b.shape[1:], jnp.float32)

                @pl.when(lat == n_lat - 1)
                def _(b=b, last=last):
                    for r in range(rows + REACH, last):
                        b[r] = jnp.zeros(b.shape[1:], jnp.float32)

            a, b = b, a
        for r in range(rows):
            out[r, :, lanes] = (scale[0:1] * a[REACH + r, pl.ds(own, across), :]).astype(jnp.bfloat16)
        return carry

    lax.fori_loop(0, tiles, tile_of, 0)


def transported(crossing, increment, multiplier, pieces, rates, token):
    rows, across, levels = increment.shape
    tall, wide, tiles = rows + 2 * REACH, across + REACH + 16, levels // LANES
    hbm, vmem = pl.BlockSpec(memory_space=pltpu.HBM), pl.BlockSpec(memory_space=pltpu.VMEM)
    return pl.pallas_call(
        functools.partial(transport_kernel, crossing),
        in_specs=[hbm, hbm] + [vmem] * (len(pieces) + 2),
        out_specs=[vmem, vmem],
        out_shape=[jax.ShapeDtypeStruct(increment.shape, jnp.bfloat16), TOKEN],
        scratch_shapes=[
            pltpu.VMEM((tiles, tall, wide, LANES), jnp.float32),
            pltpu.VMEM((tall, wide, LANES), jnp.float32),
            pltpu.SemaphoreType.DMA((tiles,)),
        ],
        compiler_params=pltpu.CompilerParams(vmem_limit_bytes=24 << 20),
        cost_estimate=pl.CostEstimate(flops=50_000_000, bytes_accessed=6 << 20, transcendentals=0),
        name="crossing" if crossing else "staying",
    )(increment, multiplier, *pieces, rates, token)


def final_kernel(inc, base, from_chip, from_core, error_out, grad_out):
    odd = lax.rem(lax.axis_index("sub"), 2) == 1
    group = 2
    for r in range(0, inc.shape[0], group):
        rows = slice(r, r + group)
        x = from_chip[rows].astype(jnp.float32)
        d = from_core[rows].astype(jnp.float32)
        error_out[rows] = inc[rows] - jnp.where(odd, d, x)
        grad_out[rows] = base[rows] - jnp.where(odd, x, d)


def final(increment, base, from_chip, from_core):
    rows, across, levels = increment.shape
    block = pl.BlockSpec((4, across, levels), lambda i: (i, 0, 0))
    return pl.pallas_call(
        final_kernel,
        grid=(rows // 4,),
        in_specs=[block] * 4,
        out_specs=[block] * 2,
        out_shape=[jax.ShapeDtypeStruct(increment.shape, jnp.float32)] * 2,
        compiler_params=pltpu.CompilerParams(vmem_limit_bytes=16 << 20),
        cost_estimate=pl.CostEstimate(flops=4_000_000, bytes_accessed=10 << 20, transcendentals=0),
        name="final",
    )(increment, base, from_chip, from_core)


ROWS_BY_COLS = (((1,), (1,)), ((), ()))


def network_kernel(
    count, columns, hidden_bias, state_in, back_in, base_in, cot_in, hidden_in, output_in,
    tangents, base_out, token,
    state, back, base, cot, hidden_weight, output_weight, sems, out_sems,
):
    cols, slots = state.shape[0], cot.shape[0]
    moves = [
        (hidden_in, hidden_weight), (back_in, back), (state_in, state),
        (output_in, output_weight), (cot_in, cot), (base_in, base),
    ]
    copies = [pltpu.make_async_copy(a, b, sems.at[i]) for i, (a, b) in enumerate(moves)]
    for copy in copies:
        copy.start()
    token[...] = jnp.zeros_like(token)
    alive = lax.broadcasted_iota(jnp.int32, (1, slots), 1) < count[0]
    named = jnp.where(alive, columns[...], -1)
    outs = []
    for i, start in enumerate(range(0, cols, COLS_TILE)):
        rows = slice(start, start + COLS_TILE)
        if i == 0:
            copies[0].wait()
            copies[1].wait()
        preact = jnp.dot(back[rows], hidden_weight[...], preferred_element_type=jnp.float32) + hidden_bias[...]
        hidden = jnp.tanh(preact)
        slopes = 1.0 - hidden * hidden
        if i == 0:
            copies[2].wait()
        forward = jnp.dot(state[rows].astype(jnp.bfloat16), hidden_weight[...], preferred_element_type=jnp.float32)
        scaled = (slopes * forward).astype(jnp.bfloat16)
        if i == 0:
            copies[3].wait()
        tangent = jnp.dot(scaled, output_weight[...], preferred_element_type=jnp.float32)
        tangents[rows] = tangent.astype(jnp.bfloat16)
        ids = lax.broadcasted_iota(jnp.int32, (COLS_TILE, slots), 0) + start
        picks = jnp.where(named == ids, 1.0, 0.0).astype(jnp.bfloat16)
        if i == 0:
            copies[4].wait()
        gathered = jnp.dot(picks, cot[...], preferred_element_type=jnp.float32).astype(jnp.bfloat16)
        pulled = lax.dot_general(gathered, output_weight[...], ROWS_BY_COLS, preferred_element_type=jnp.float32)
        weighted = (slopes * pulled).astype(jnp.bfloat16)
        adjoint = lax.dot_general(weighted, hidden_weight[...], ROWS_BY_COLS, preferred_element_type=jnp.float32)
        if i == 0:
            copies[5].wait()
        base[rows] = base[rows] + adjoint
        outs.append(pltpu.make_async_copy(base.at[rows], base_out.at[rows], out_sems.at[i]))
        outs[-1].start()
    for out in outs:
        out.wait()


def network(count, columns, state, back, base, cot, hidden_weight, hidden_bias, output_weight):
    cols, levels = state.shape
    slots, chan = cot.shape
    hbm, vmem = pl.BlockSpec(memory_space=pltpu.HBM), pl.BlockSpec(memory_space=pltpu.VMEM)
    moved = (state, back, base, cot, hidden_weight, output_weight)
    return pl.pallas_call(
        network_kernel,
        in_specs=[pl.BlockSpec(memory_space=pltpu.SMEM), vmem, vmem] + [hbm] * 6,
        out_specs=[vmem, hbm, vmem],
        out_shape=[
            jax.ShapeDtypeStruct((cols, chan), jnp.bfloat16),
            jax.ShapeDtypeStruct((cols, levels), jnp.float32),
            TOKEN,
        ],
        scratch_shapes=[pltpu.VMEM(a.shape, a.dtype) for a in moved]
        + [pltpu.SemaphoreType.DMA((6,)), pltpu.SemaphoreType.DMA((cols // COLS_TILE,))],
        cost_estimate=pl.CostEstimate(
            flops=2 * (5 * cols + slots) * levels * hidden_bias.shape[1],
            bytes_accessed=12 << 20,
            transcendentals=1 << 20,
        ),
        name="network",
    )(count, columns, hidden_bias, *moved)


def spread_kernel(count, columns, tangents, _, out, token, held, sems):
    slots, cols = held.shape[0], tangents.shape[0]
    token[...] = jnp.zeros_like(token)
    lane = lax.broadcasted_iota(jnp.int32, (LANES, LANES), 1)
    outs = []
    for i, start in enumerate(range(0, slots, SLOTS_TILE)):
        rows = slice(start, start + SLOTS_TILE)
        parts = []
        for s in range(start, start + SLOTS_TILE, LANES):
            alive = lax.broadcasted_iota(jnp.int32, (1, LANES), 1) + s < count[0]
            named = jnp.where(alive, columns[:, s : s + LANES], -1)
            mine = jnp.broadcast_to(named, (LANES, LANES)).T
            hits = [jnp.where(mine == lane + k, 1.0, 0.0).astype(jnp.bfloat16) for k in range(0, cols, LANES)]
            parts.append(jnp.concatenate(hits, axis=1))
        picks = jnp.concatenate(parts, axis=0)
        held[rows] = jnp.dot(picks, tangents[...], preferred_element_type=jnp.float32).astype(jnp.bfloat16)
        outs.append(pltpu.make_async_copy(held.at[rows], out.at[rows], sems.at[i]))
        outs[-1].start()
    for copy in outs:
        copy.wait()


def spread(count, columns, tangents, token):
    slots, (cols, chan) = columns.shape[1], tangents.shape
    vmem = pl.BlockSpec(memory_space=pltpu.VMEM)
    return pl.pallas_call(
        spread_kernel,
        in_specs=[pl.BlockSpec(memory_space=pltpu.SMEM), vmem, vmem, vmem],
        out_specs=[pl.BlockSpec(memory_space=pltpu.HBM), vmem],
        out_shape=[jax.ShapeDtypeStruct((slots, chan), jnp.bfloat16), TOKEN],
        scratch_shapes=[
            pltpu.VMEM((slots, chan), jnp.bfloat16),
            pltpu.SemaphoreType.DMA((slots // SLOTS_TILE,)),
        ],
        compiler_params=pltpu.CompilerParams(vmem_limit_bytes=24 << 20),
        cost_estimate=pl.CostEstimate(flops=2 * slots * cols * chan, bytes_accessed=4 << 20, transcendentals=0),
        name="spread",
    )(count, columns, tangents, token)


def sent(array, to):
    counts = [lax.axis_size(axis) for axis in ("sub", "lat", "lon")]
    flat = lambda s, a, o: (s * counts[1] + a) * counts[2] + o
    pairs = []
    for s in range(counts[0]):
        for a in range(counts[1]):
            for o in range(counts[2]):
                target = to(s, a, o)
                if all(0 <= t < n for t, n in zip(target, counts)):
                    pairs.append((flat(s, a, o), flat(*target)))
    return lax.ppermute(array, ("sub", "lat", "lon"), pairs)


def local(
    increment,
    multiplier,
    background,
    obs_cotangent,
    obs_column,
    obs_count,
    transport,
    hidden_weight,
    hidden_bias,
    output_weight,
):
    increment, multiplier = increment[0], multiplier[0]
    levels = increment.shape[2]
    low, high, strip = pack(increment, multiplier)
    across = sent(strip, lambda s, a, o: (s, a, 1 - o))
    above = sent(high, lambda s, a, o: (s, a + 1, o))
    below = sent(low, lambda s, a, o: (s, a - 1, o))
    myself = lax.axis_index(("lat", "lon"))
    my_count = lax.dynamic_slice(obs_count[0], (myself,), (1,))
    tangents, base, token = network(
        my_count,
        obs_column[0],
        increment.reshape(-1, levels),
        background[0].reshape(-1, levels),
        multiplier.reshape(-1, levels),
        obs_cotangent[0, 0],
        hidden_weight,
        hidden_bias[None, :],
        output_weight,
    )
    low_corner, high_corner, token = corners(across, token)
    above_corner = sent(high_corner, lambda s, a, o: (s, a + 1, o))
    below_corner = sent(low_corner, lambda s, a, o: (s, a - 1, o))
    tangent, token = spread(my_count, obs_column[0], tangents, token)
    pieces = [above, below, across, above_corner, below_corner]
    crossing, token = transported(True, increment, multiplier, pieces, transport, token)
    from_chip = sent(crossing, lambda s, a, o: (s + 1 if s % 2 else s - 1, a, o))
    staying, _ = transported(False, increment, multiplier, pieces, transport, token)
    from_core = sent(staying, lambda s, a, o: (s - 1 if s % 2 else s + 1, a, o))
    model_error, gradient = final(increment, base.reshape(increment.shape), from_chip, from_core)
    return (model_error[None], gradient[None], tangent[None, None])


def solution(mesh):
    in_specs = (
        P("sub", "lat", "lon", None),
        P("sub", "lat", "lon", None),
        P("sub", "lat", "lon", None),
        P("sub", ("lat", "lon"), None, None),
        P("sub", ("lat", "lon"), None),
        P("sub", None),
        P(),
        P(),
        P(),
        P(),
    )
    out_specs = (
        P("sub", "lat", "lon", None),
        P("sub", "lat", "lon", None),
        P("sub", ("lat", "lon"), None, None),
    )
    return jax.shard_map(local, mesh=mesh, in_specs=in_specs, out_specs=out_specs, check_vma=False)
```

profile of v0, /device:TPU:11, one launch (start us, length us, event | category | flops | bytes accessed | tf_op | source)
XLA Modules:
  0.0 84.5 jit_solution(17793183661371025721)
XLA Ops:
  0.6 0.0 copy-start
  0.6 3.6 %pack.1 = (bf16[2,8,64,512]{3,2,1,0:T(8,128)(2,1)}, bf16[2,8,64,512]{3,2,1,0:T(8,128)(2,1)}, bf16[2,16,8,512]{3,2,1,0:T(8,128)(2,1)}) custom-call(f32[16,64,512]{2,1,0:T(8,128)} %bitcast.13, f32[16,64,512]{2,1,0:T(8,128)} %bitcast.18), custom_call_target="tpu_custom_call" | custom-call | tf_op jit(solution)/shard_map/pack/pallas_call | solution.py:49
  4.3 3.5 %collective-permute-start = (bf16[2,8,64,512]{3,2,1,0:T(8,128)(2,1)}, bf16[2,8,64,512]{3,2,1,0:T(8,128)(2,1)S(1)}, u32[]{:S(2)}, u32[]{:S(2)}) collective-permute-start(bf16[2,8,64,512]{3,2,1,0:T(8,128)(2,1)} %get-tuple-element.20), channel_id=1, source_target_pairs={{0,2},{1,3},{2,4},{3,5},{4,6},{5,7},{6,8},{7,9},{8,10},{9,11},{10,... | collective-permute-start | bytes 3145736 | tf_op jit(solution)/shard_map/ppermute | solution.py:365
  7.8 3.9 %collective-permute-start.1 = (bf16[2,8,64,512]{3,2,1,0:T(8,128)(2,1)}, bf16[2,8,64,512]{3,2,1,0:T(8,128)(2,1)S(1)}, u32[]{:S(2)}, u32[]{:S(2)}) collective-permute-start(bf16[2,8,64,512]{3,2,1,0:T(8,128)(2,1)} %get-tuple-element.21), channel_id=1, source_target_pairs={{2,0},{3,1},{4,2},{5,3},{6,4},{7,5},{8,6},{9,7},{10,8},{11,9},{12,... | collective-permute-start | bytes 3145736 | tf_op jit(solution)/shard_map/ppermute | solution.py:365
  11.8 2.4 %collective-permute-start.2 = (bf16[2,16,8,512]{3,2,1,0:T(8,128)(2,1)}, bf16[2,16,8,512]{3,2,1,0:T(8,128)(2,1)S(1)}, u32[]{:S(2)}, u32[]{:S(2)}) collective-permute-start(bf16[2,16,8,512]{3,2,1,0:T(8,128)(2,1)} %get-tuple-element.22), channel_id=1, source_target_pairs={{0,1},{1,0},{2,3},{3,2},{4,5},{5,4},{6,7},{7,6},{8,9},{9,8},{10,11... | collective-permute-start | bytes 786440 | tf_op jit(solution)/shard_map/ppermute | solution.py:365
  14.1 0.0 copy-done
  14.1 0.6 constant_dynamic-slice_fusion
  14.7 14.0 %network.1 = (bf16[1024,512]{1,0:T(8,128)(2,1)}, f32[1024,512]{1,0:T(8,128)}, f32[8,128]{1,0:T(8,128)}) custom-call(s32[1]{0:T(128)} %bitcast.1.count, s32[1,2048]{1,0:T(1,128)} %bitcast.23, f32[1,1024]{1,0:T(1,128)} %bitcast.29, f32[1024,512]{1,0:T(8,128)} %bitcast.14, bf16[1024,512]{1,0:T(8,128)(2,1)} %bitcast.28, f32[1024,512]{1,0:T(8,128)} %bitcast.19, ...), custom_call_target="tpu_custom_call" | custom-call | flops 7516192768 | bytes 12582912 | tf_op jit(solution)/shard_map/network/pallas_call | solution.py:295
  28.8 13.7 %collective-permute-done.2.strip = bf16[2,16,8,512]{3,2,1,0:T(8,128)(2,1)S(1)} collective-permute-done((bf16[2,16,8,512]{3,2,1,0:T(8,128)(2,1)}, bf16[2,16,8,512]{3,2,1,0:T(8,128)(2,1)S(1)}, u32[]{:S(2)}, u32[]{:S(2)}) %collective-permute-start.2) | collective-permute-done | bytes 262176 | tf_op jit(solution)/shard_map/ppermute | solution.py:365
  42.4 0.7 copy-done.5
  43.1 1.9 %collective-permute-start.3 = (bf16[2,6,8,512]{3,2,1,0:T(8,128)(2,1)S(1)}, bf16[2,6,8,512]{3,2,1,0:T(8,128)(2,1)S(1)}, u32[]{:S(2)}, u32[]{:S(2)}) collective-permute-start(bf16[2,6,8,512]{3,2,1,0:T(8,128)(2,1)S(1)} %get-tuple-element.24), channel_id=1, source_target_pairs={{0,2},{1,3},{2,4},{3,5},{4,6},{5,7},{6,8},{7,9},{8,10},{9,11},{10,... | collective-permute-start | bytes 294920 | tf_op jit(solution)/shard_map/ppermute | solution.py:365
  45.1 5.5 %collective-permute-start.4 = (bf16[2,6,8,512]{3,2,1,0:T(8,128)(2,1)S(1)}, bf16[2,6,8,512]{3,2,1,0:T(8,128)(2,1)S(1)}, u32[]{:S(2)}, u32[]{:S(2)}) collective-permute-start(bf16[2,6,8,512]{3,2,1,0:T(8,128)(2,1)S(1)} %get-tuple-element.25), channel_id=1, source_target_pairs={{2,0},{3,1},{4,2},{5,3},{6,4},{7,5},{8,6},{9,7},{10,8},{11,9},{12,... | collective-permute-start | bytes 294920 | tf_op jit(solution)/shard_map/ppermute | solution.py:365
  50.5 0.0 copy-done.6
  50.6 0.0 copy-start.7
  50.6 1.2 %copy-done.7 = bf16[1024,512]{1,0:T(8,128)(2,1)S(1)} copy-done((bf16[1024,512]{1,0:T(8,128)(2,1)S(1)}, bf16[1024,512]{1,0:T(8,128)(2,1)}, u32[]{:S(2)}) %copy-start.7) | copy-done | bytes 1048600
  51.8 4.0 %spread.1 = (bf16[2048,512]{1,0:T(8,128)(2,1)}, f32[8,128]{1,0:T(8,128)S(1)}) custom-call(s32[1]{0:T(128)} %bitcast.1.count, s32[1,2048]{1,0:T(1,128)S(1)} %bitcast.24, bf16[1024,512]{1,0:T(8,128)(2,1)S(1)} %copy-done.7, f32[8,128]{1,0:T(8,128)S(1)} %get-tuple-element.27._), custom_call_target="tpu_custom_call" | custom-call | flops 2147483648 | bytes 4194304 | tf_op jit(solution)/shard_map/spread/pallas_call | solution.py:340
  55.8 0.0 collective-permute-done.3.above_corner
  55.8 0.0 collective-permute-done.4.below_corner
  55.8 0.0 collective-permute-done.above
  55.8 0.0 collective-permute-done.1.below
  55.8 0.0 copy-done.1
  55.8 0.0 copy-done.2
  55.9 0.0 copy-done.4
  55.9 8.2 %crossing.1 = (bf16[16,64,512]{2,1,0:T(8,128)(2,1)S(1)}, f32[8,128]{1,0:T(8,128)S(1)}) custom-call(f32[16,64,512]{2,1,0:T(8,128)S(1)} %bitcast.15, f32[16,64,512]{2,1,0:T(8,128)S(1)} %bitcast.20, bf16[2,8,64,512]{3,2,1,0:T(8,128)(2,1)S(1)} %collective-permute-done.above, bf16[2,8,64,512]{3,2,1,0:T(8,128)(2,1)S(1)} %collective-permute-done.1.below, ...), custom_call_target="tpu_custom_call" | custom-call | flops 50000000 | bytes 6291456 | tf_op jit(solution)/shard_map/crossing/pallas_call | solution.py:195
  64.1 5.1 %collective-permute-start.5 = (bf16[16,64,512]{2,1,0:T(8,128)(2,1)S(1)}, bf16[16,64,512]{2,1,0:T(8,128)(2,1)S(1)}, u32[]{:S(2)}, u32[]{:S(2)}) collective-permute-start(bf16[16,64,512]{2,1,0:T(8,128)(2,1)S(1)} %get-tuple-element.29), channel_id=1, source_target_pairs={{16,32},{17,33},{18,34},{19,35},{20,36},{21,37},{22,38},{23,39},{2... | collective-permute-start | bytes 3145736 | tf_op jit(solution)/shard_map/ppermute | solution.py:365
  69.2 0.0 copy-start.3
  69.2 8.8 %staying.1 = (bf16[16,64,512]{2,1,0:T(8,128)(2,1)S(1)}, f32[8,128]{1,0:T(8,128)}) custom-call(f32[16,64,512]{2,1,0:T(8,128)S(1)} %bitcast.16, f32[16,64,512]{2,1,0:T(8,128)S(1)} %bitcast.21, bf16[2,8,64,512]{3,2,1,0:T(8,128)(2,1)S(1)} %collective-permute-done.above, bf16[2,8,64,512]{3,2,1,0:T(8,128)(2,1)S(1)} %collective-permute-done.1.below, ...), custom_call_target="tpu_custom_call" | custom-call | flops 50000000 | bytes 6291456 | tf_op jit(solution)/shard_map/staying/pallas_call | solution.py:195
  78.0 0.1 collective-permute-start.6
  78.1 3.8 %collective-permute-done.5.from_chip = bf16[16,64,512]{2,1,0:T(8,128)(2,1)S(1)} collective-permute-done((bf16[16,64,512]{2,1,0:T(8,128)(2,1)S(1)}, bf16[16,64,512]{2,1,0:T(8,128)(2,1)S(1)}, u32[]{:S(2)}, u32[]{:S(2)}) %collective-permute-start.5) | collective-permute-done | bytes 1048608 | tf_op jit(solution)/shard_map/ppermute | solution.py:365
  81.9 0.0 collective-permute-done.6.from_core
  81.9 0.0 copy-done.3
  81.9 2.6 %final.1 = (f32[16,64,512]{2,1,0:T(8,128)}, f32[16,64,512]{2,1,0:T(8,128)}) custom-call(f32[16,64,512]{2,1,0:T(8,128)S(1)} %bitcast.17, f32[16,64,512]{2,1,0:T(8,128)S(1)} %bitcast.22, bf16[16,64,512]{2,1,0:T(8,128)(2,1)S(1)} %collective-permute-done.5.from_chip, bf16[16,64,512]{2,1,0:T(8,128)(2,1)S(1)} %collective-permute-done.6.from_core), custom_call_target="tpu_custom_call" | custom-call | flops 4000000 | bytes 10485760 | tf_op jit(solution)/shard_map/final/pallas_call | solution.py:225
  (6 shorter events, 0.0 us)
Async XLA Ops:
  0.6 13.5 %copy-start = (s32[1,16]{1,0:T(1,128)S(1)}, s32[1,16]{1,0:T(1,128)}, u32[]{:S(2)}) copy-start(s32[1,16]{1,0:T(1,128)} %param.15) | copy-start | bytes 196
  4.3 51.6 %collective-permute-start = (bf16[2,8,64,512]{3,2,1,0:T(8,128)(2,1)}, bf16[2,8,64,512]{3,2,1,0:T(8,128)(2,1)S(1)}, u32[]{:S(2)}, u32[]{:S(2)}) collective-permute-start(bf16[2,8,64,512]{3,2,1,0:T(8,128)(2,1)} %get-tuple-element.20), channel_id=1, source_target_pairs={{0,2},{1,3},{2,4},{3,5},{4,6},{5,7},{6,8},{7,9},{8,10},{9,11},{10,... | collective-permute-start | bytes 3145736 | tf_op jit(solution)/shard_map/ppermute | solution.py:365
  7.8 48.0 %collective-permute-start.1 = (bf16[2,8,64,512]{3,2,1,0:T(8,128)(2,1)}, bf16[2,8,64,512]{3,2,1,0:T(8,128)(2,1)S(1)}, u32[]{:S(2)}, u32[]{:S(2)}) collective-permute-start(bf16[2,8,64,512]{3,2,1,0:T(8,128)(2,1)} %get-tuple-element.21), channel_id=1, source_target_pairs={{2,0},{3,1},{4,2},{5,3},{6,4},{7,5},{8,6},{9,7},{10,8},{11,9},{12,... | collective-permute-start | bytes 3145736 | tf_op jit(solution)/shard_map/ppermute | solution.py:365
  11.8 30.7 %collective-permute-start.2 = (bf16[2,16,8,512]{3,2,1,0:T(8,128)(2,1)}, bf16[2,16,8,512]{3,2,1,0:T(8,128)(2,1)S(1)}, u32[]{:S(2)}, u32[]{:S(2)}) collective-permute-start(bf16[2,16,8,512]{3,2,1,0:T(8,128)(2,1)} %get-tuple-element.22), channel_id=1, source_target_pairs={{0,1},{1,0},{2,3},{3,2},{4,5},{5,4},{6,7},{7,6},{8,9},{9,8},{10,11... | collective-permute-start | bytes 786440 | tf_op jit(solution)/shard_map/ppermute | solution.py:365
  14.7 35.8 %copy-start.6 = (s32[1,1,2048]{2,1,0:T(1,128)S(1)}, s32[1,1,2048]{2,1,0:T(1,128)}, u32[]{:S(2)}) copy-start(s32[1,1,2048]{2,1,0:T(1,128)} %param.14) | copy-start | bytes 24580
  42.4 0.7 copy-start.5
  43.1 12.7 %collective-permute-start.3 = (bf16[2,6,8,512]{3,2,1,0:T(8,128)(2,1)S(1)}, bf16[2,6,8,512]{3,2,1,0:T(8,128)(2,1)S(1)}, u32[]{:S(2)}, u32[]{:S(2)}) collective-permute-start(bf16[2,6,8,512]{3,2,1,0:T(8,128)(2,1)S(1)} %get-tuple-element.24), channel_id=1, source_target_pairs={{0,2},{1,3},{2,4},{3,5},{4,6},{5,7},{6,8},{7,9},{8,10},{9,11},{10,... | collective-permute-start | bytes 294920 | tf_op jit(solution)/shard_map/ppermute | solution.py:365
  45.1 10.7 %collective-permute-start.4 = (bf16[2,6,8,512]{3,2,1,0:T(8,128)(2,1)S(1)}, bf16[2,6,8,512]{3,2,1,0:T(8,128)(2,1)S(1)}, u32[]{:S(2)}, u32[]{:S(2)}) collective-permute-start(bf16[2,6,8,512]{3,2,1,0:T(8,128)(2,1)S(1)} %get-tuple-element.25), channel_id=1, source_target_pairs={{2,0},{3,1},{4,2},{5,3},{6,4},{7,5},{8,6},{9,7},{10,8},{11,9},{12,... | collective-permute-start | bytes 294920 | tf_op jit(solution)/shard_map/ppermute | solution.py:365
  50.6 1.2 %copy-start.7 = (bf16[1024,512]{1,0:T(8,128)(2,1)S(1)}, bf16[1024,512]{1,0:T(8,128)(2,1)}, u32[]{:S(2)}) copy-start(bf16[1024,512]{1,0:T(8,128)(2,1)} %get-tuple-element.26.tangents) | copy-start | bytes 3145732
  51.8 4.1 %copy-start.1 = (f32[1,16,64,512]{3,2,1,0:T(8,128)S(1)}, f32[1,16,64,512]{3,2,1,0:T(8,128)}, u32[]{:S(2)}) copy-start(f32[1,16,64,512]{3,2,1,0:T(8,128)} %param.10) | copy-start | bytes 6291460
  51.8 4.1 %copy-start.2 = (f32[1,16,64,512]{3,2,1,0:T(8,128)S(1)}, f32[1,16,64,512]{3,2,1,0:T(8,128)}, u32[]{:S(2)}) copy-start(f32[1,16,64,512]{3,2,1,0:T(8,128)} %param.11) | copy-start | bytes 6291460
  51.8 4.1 %copy-start.4 = (f32[8,512]{1,0:T(8,128)S(1)}, f32[8,512]{1,0:T(8,128)}, u32[]{:S(2)}) copy-start(f32[8,512]{1,0:T(8,128)} %rates.3) | copy-start | bytes 49156
  64.1 17.8 %collective-permute-start.5 = (bf16[16,64,512]{2,1,0:T(8,128)(2,1)S(1)}, bf16[16,64,512]{2,1,0:T(8,128)(2,1)S(1)}, u32[]{:S(2)}, u32[]{:S(2)}) collective-permute-start(bf16[16,64,512]{2,1,0:T(8,128)(2,1)S(1)} %get-tuple-element.29), channel_id=1, source_target_pairs={{16,32},{17,33},{18,34},{19,35},{20,36},{21,37},{22,38},{23,39},{2... | collective-permute-start | bytes 3145736 | tf_op jit(solution)/shard_map/ppermute | solution.py:365
  69.2 12.7 %copy-start.3 = (f32[1024,512]{1,0:T(8,128)S(1)}, f32[1024,512]{1,0:T(8,128)}, u32[]{:S(2)}) copy-start(f32[1024,512]{1,0:T(8,128)} %get-tuple-element.19) | copy-start | bytes 6291460
  78.0 3.9 %collective-permute-start.6 = (bf16[16,64,512]{2,1,0:T(8,128)(2,1)S(1)}, bf16[16,64,512]{2,1,0:T(8,128)(2,1)S(1)}, u32[]{:S(2)}, u32[]{:S(2)}) collective-permute-start(bf16[16,64,512]{2,1,0:T(8,128)(2,1)S(1)} %get-tuple-element.31), channel_id=1, source_target_pairs={{0,16},{1,17},{2,18},{3,19},{4,20},{5,21},{6,22},{7,23},{8,24},{9,... | collective-permute-start | bytes 3145736 | tf_op jit(solution)/shard_map/ppermute | solution.py:365
where the time goes:
time: 84.8 us; the launch traced here: 84.5 us
  Pallas kernels  41.2 us (49%)
  starting transfers between devices  22.4 us (26%)
  waiting for transfers between devices  17.5 us (21%)
  local copies, waits for them, and re-layouts  2.52 us (3%)
    ppermute x7, starting transfers between devices, sent(): return lax.ppermute(array, ('sub', 'lat', 'lon'), pairs)  22.4 us
    ppermute x7, waiting for transfers between devices, sent(): return lax.ppermute(array, ('sub', 'lat', 'lon'), pairs)  17.5 us
    pallas_call x2, Pallas kernels, transported(): pl.pallas_call(functools.partial(transport_kernel, crossing), in_specs=[h...  17 us
    pallas_call x1, Pallas kernels, network(): pl.pallas_call(network_kernel, in_specs=[pl.BlockSpec(memory_space=pltpu....  14 us
    pallas_call x1, Pallas kernels, spread(): pl.pallas_call(spread_kernel, in_specs=[pl.BlockSpec(memory_space=pltpu.S...  4 us
    pallas_call x1, Pallas kernels, pack(): pl.pallas_call(pack_kernel, in_specs=[pl.BlockSpec(memory_space=pltpu.HBM...  3.61 us
    pallas_call x1, Pallas kernels, final(): pl.pallas_call(final_kernel, grid=(rows // 4,), in_specs=[block] * 4, out...  2.55 us
    unnamed x16, local copies, waits for them, and re-layouts  1.92 us
  transfers between devices with their start and end apart: 7, of which 2 were waited for; matrix products, arithmetic and copies ran while one was open for 1% of the time, Pallas kernels for 32%

commit v1 on v0

--- a/solution.py
+++ b/solution.py
@@ -19,6 +19,10 @@
 
 
 CHUNK = 4
+
+
+def in_hbm(*arrays):
+    return [pltpu.with_memory_space_constraint(a, pltpu.HBM) for a in arrays]
 
 
 def pack_kernel(inc, mul, low, high, strip, held, sems):
@@ -55,8 +59,9 @@
             pltpu.VMEM((2,) + increment.shape, jnp.float32),
             pltpu.SemaphoreType.DMA((2, rows // CHUNK)),
         ],
+        compiler_params=pltpu.CompilerParams(vmem_limit_bytes=16 << 20),
         name="pack",
-    )(increment, multiplier)
+    )(*in_hbm(increment, multiplier))
 
 
 def corner_kernel(strip, _, low, high, token):
@@ -70,6 +75,7 @@
     fields, _, wide, levels = strip.shape
     return pl.pallas_call(
         corner_kernel,
+        in_specs=[pl.BlockSpec(memory_space=pltpu.VMEM), pl.BlockSpec(memory_space=pl.ANY)],
         out_shape=[jax.ShapeDtypeStruct((fields, EDGE, wide, levels), jnp.bfloat16)] * 2 + [TOKEN],
         compiler_params=pltpu.CompilerParams(vmem_limit_bytes=8 << 20),
         name="corners",
@@ -194,7 +200,7 @@
     hbm, vmem = pl.BlockSpec(memory_space=pltpu.HBM), pl.BlockSpec(memory_space=pltpu.VMEM)
     return pl.pallas_call(
         functools.partial(transport_kernel, crossing),
-        in_specs=[hbm, hbm] + [vmem] * (len(pieces) + 2),
+        in_specs=[hbm, hbm] + [vmem] * (len(pieces) + 1) + [pl.BlockSpec(memory_space=pl.ANY)],
         out_specs=[vmem, vmem],
         out_shape=[jax.ShapeDtypeStruct(increment.shape, jnp.bfloat16), TOKEN],
         scratch_shapes=[
@@ -205,7 +211,7 @@
         compiler_params=pltpu.CompilerParams(vmem_limit_bytes=24 << 20),
         cost_estimate=pl.CostEstimate(flops=50_000_000, bytes_accessed=6 << 20, transcendentals=0),
         name="crossing" if crossing else "staying",
-    )(increment, multiplier, *pieces, rates, token)
+    )(*in_hbm(increment, multiplier), *pieces, rates, token)
 
 
 def final_kernel(inc, base, from_chip, from_core, error_out, grad_out):
@@ -308,13 +314,13 @@
             bytes_accessed=12 << 20,
             transcendentals=1 << 20,
         ),
+        compiler_params=pltpu.CompilerParams(vmem_limit_bytes=40 << 20),
         name="network",
-    )(count, columns, hidden_bias, *moved)
-
-
-def spread_kernel(count, columns, tangents, _, out, token, held, sems):
+    )(count, columns, hidden_bias, *in_hbm(*moved))
+
+
+def spread_kernel(count, columns, tangents, _, out, held, sems):
     slots, cols = held.shape[0], tangents.shape[0]
-    token[...] = jnp.zeros_like(token)
     lane = lax.broadcasted_iota(jnp.int32, (LANES, LANES), 1)
     outs = []
     for i, start in enumerate(range(0, slots, SLOTS_TILE)):
@@ -339,9 +345,9 @@
     vmem = pl.BlockSpec(memory_space=pltpu.VMEM)
     return pl.pallas_call(
         spread_kernel,
-        in_specs=[pl.BlockSpec(memory_space=pltpu.SMEM), vmem, vmem, vmem],
-        out_specs=[pl.BlockSpec(memory_space=pltpu.HBM), vmem],
-        out_shape=[jax.ShapeDtypeStruct((slots, chan), jnp.bfloat16), TOKEN],
+        in_specs=[pl.BlockSpec(memory_space=pltpu.SMEM), vmem, vmem, pl.BlockSpec(memory_space=pl.ANY)],
+        out_specs=pl.BlockSpec(memory_space=pltpu.HBM),
+        out_shape=jax.ShapeDtypeStruct((slots, chan), jnp.bfloat16),
         scratch_shapes=[
             pltpu.VMEM((slots, chan), jnp.bfloat16),
             pltpu.SemaphoreType.DMA((slots // SLOTS_TILE,)),
@@ -380,9 +386,9 @@
     increment, multiplier = increment[0], multiplier[0]
     levels = increment.shape[2]
     low, high, strip = pack(increment, multiplier)
-    across = sent(strip, lambda s, a, o: (s, a, 1 - o))
     above = sent(high, lambda s, a, o: (s, a + 1, o))
     below = sent(low, lambda s, a, o: (s, a - 1, o))
+    across = sent(strip, lambda s, a, o: (s, a, 1 - o))
     myself = lax.axis_index(("lat", "lon"))
     my_count = lax.dynamic_slice(obs_count[0], (myself,), (1,))
     tangents, base, token = network(
@@ -399,12 +405,12 @@
     low_corner, high_corner, token = corners(across, token)
     above_corner = sent(high_corner, lambda s, a, o: (s, a + 1, o))
     below_corner = sent(low_corner, lambda s, a, o: (s, a - 1, o))
-    tangent, token = spread(my_count, obs_column[0], tangents, token)
     pieces = [above, below, across, above_corner, below_corner]
     crossing, token = transported(True, increment, multiplier, pieces, transport, token)
     from_chip = sent(crossing, lambda s, a, o: (s + 1 if s % 2 else s - 1, a, o))
-    staying, _ = transported(False, increment, multiplier, pieces, transport, token)
+    staying, token = transported(False, increment, multiplier, pieces, transport, token)
     from_core = sent(staying, lambda s, a, o: (s - 1 if s % 2 else s + 1, a, o))
+    tangent = spread(my_count, obs_column[0], tangents, token)
     model_error, gradient = final(increment, base.reshape(increment.shape), from_chip, from_core)
     return (model_error[None], gradient[None], tangent[None, None])
 

time: 84.8 us -> 81.7 us (0.963)
  the two profiles are of different devices: /device:TPU:11 before, /device:TPU:97 now
where the time goes in v1:
time: 81.7 us; the launch traced here: 81.4 us
  Pallas kernels  39.3 us (48%)
  starting transfers between devices  22.6 us (28%)
  waiting for transfers between devices  18.1 us (22%)
    ppermute x7, starting transfers between devices, sent(): return lax.ppermute(array, ('sub', 'lat', 'lon'), pairs)  22.6 us
    ppermute x7, waiting for transfers between devices, sent(): return lax.ppermute(array, ('sub', 'lat', 'lon'), pairs)  18.1 us
    pallas_call x2, Pallas kernels, transported(): pl.pallas_call(functools.partial(transport_kernel, crossing), in_specs=[h...  17.3 us
    pallas_call x1, Pallas kernels, network(): pl.pallas_call(network_kernel, in_specs=[pl.BlockSpec(memory_space=pltpu....  12.1 us
    pallas_call x1, Pallas kernels, spread(): pl.pallas_call(spread_kernel, in_specs=[pl.BlockSpec(memory_space=pltpu.S...  4.02 us
    pallas_call x1, Pallas kernels, pack(): pl.pallas_call(pack_kernel, in_specs=[pl.BlockSpec(memory_space=pltpu.HBM...  3.31 us
    pallas_call x1, Pallas kernels, final(): pl.pallas_call(final_kernel, grid=(rows // 4,), in_specs=[block] * 4, out...  2.56 us
  transfers between devices with their start and end apart: 7, of which 2 were waited for; matrix products, arithmetic and copies ran while one was open for 1% of the time, Pallas kernels for 30%

profile of v1, /device:TPU:97, one launch (start us, length us, event | category | flops | bytes accessed | tf_op | source)
XLA Modules:
  0.0 81.4 jit_solution(8921313852710994411)
XLA Ops:
  0.6 0.0 copy-start
  0.6 0.0 copy-start.3
  0.7 0.0 copy-start.4
  0.7 3.3 %pack.1 = (bf16[2,8,64,512]{3,2,1,0:T(8,128)(2,1)S(1)}, bf16[2,8,64,512]{3,2,1,0:T(8,128)(2,1)}, bf16[2,16,8,512]{3,2,1,0:T(8,128)(2,1)}) custom-call(f32[16,64,512]{2,1,0:T(8,128)} %bitcast.13, f32[16,64,512]{2,1,0:T(8,128)} %bitcast.22), custom_call_target="tpu_custom_call" | custom-call | tf_op jit(solution)/shard_map/pack/pallas_call | solution.py:53
  4.0 1.9 %collective-permute-start = (bf16[2,8,64,512]{3,2,1,0:T(8,128)(2,1)}, bf16[2,8,64,512]{3,2,1,0:T(8,128)(2,1)S(1)}, u32[]{:S(2)}, u32[]{:S(2)}) collective-permute-start(bf16[2,8,64,512]{3,2,1,0:T(8,128)(2,1)} %get-tuple-element.19), channel_id=1, source_target_pairs={{0,2},{1,3},{2,4},{3,5},{4,6},{5,7},{6,8},{7,9},{8,10},{9,11},{10,... | collective-permute-start | bytes 3145736 | tf_op jit(solution)/shard_map/ppermute | solution.py:371
  5.9 3.4 %collective-permute-start.1 = (bf16[2,8,64,512]{3,2,1,0:T(8,128)(2,1)S(1)}, bf16[2,8,64,512]{3,2,1,0:T(8,128)(2,1)S(1)}, u32[]{:S(2)}, u32[]{:S(2)}) collective-permute-start(bf16[2,8,64,512]{3,2,1,0:T(8,128)(2,1)S(1)} %get-tuple-element.20), channel_id=1, source_target_pairs={{2,0},{3,1},{4,2},{5,3},{6,4},{7,5},{8,6},{9,7},{10,8},{11,9},{12,... | collective-permute-start | bytes 3145736 | tf_op jit(solution)/shard_map/ppermute | solution.py:371
  9.3 3.0 %collective-permute-start.2 = (bf16[2,16,8,512]{3,2,1,0:T(8,128)(2,1)}, bf16[2,16,8,512]{3,2,1,0:T(8,128)(2,1)S(1)}, u32[]{:S(2)}, u32[]{:S(2)}) collective-permute-start(bf16[2,16,8,512]{3,2,1,0:T(8,128)(2,1)} %get-tuple-element.21), channel_id=1, source_target_pairs={{0,1},{1,0},{2,3},{3,2},{4,5},{5,4},{6,7},{7,6},{8,9},{9,8},{10,11... | collective-permute-start | bytes 786440 | tf_op jit(solution)/shard_map/ppermute | solution.py:371
  12.3 0.0 copy-done
  12.3 0.6 constant_dynamic-slice_fusion
  12.9 0.0 copy-done.3
  12.9 0.0 copy-done.4
  12.9 0.0 copy-start.2
  12.9 12.1 %network.1 = (bf16[1024,512]{1,0:T(8,128)(2,1)S(1)}, f32[1024,512]{1,0:T(8,128)S(1)}, f32[8,128]{1,0:T(8,128)S(1)}) custom-call(s32[1]{0:T(128)} %bitcast.1.count, s32[1,2048]{1,0:T(1,128)S(1)} %bitcast.19, f32[1,1024]{1,0:T(1,128)S(1)} %bitcast.21, f32[1024,512]{1,0:T(8,128)} %bitcast.14, bf16[1024,512]{1,0:T(8,128)(2,1)} %bitcast.29, ...), custom_call_target="tpu_custom_call" | custom-call | flops 7516192768 | bytes 12582912 | tf_op jit(solution)/shard_map/network/pallas_call | solution.py:301
  25.0 12.5 %collective-permute-done.2.strip = bf16[2,16,8,512]{3,2,1,0:T(8,128)(2,1)S(1)} collective-permute-done((bf16[2,16,8,512]{3,2,1,0:T(8,128)(2,1)}, bf16[2,16,8,512]{3,2,1,0:T(8,128)(2,1)S(1)}, u32[]{:S(2)}, u32[]{:S(2)}) %collective-permute-start.2) | collective-permute-done | bytes 262176 | tf_op jit(solution)/shard_map/ppermute | solution.py:371
  37.5 6.3 %collective-permute-start.3 = (bf16[2,6,8,512]{3,2,1,0:T(8,128)(2,1)S(1)}, bf16[2,6,8,512]{3,2,1,0:T(8,128)(2,1)S(1)}, u32[]{:S(2)}, u32[]{:S(2)}) collective-permute-start(bf16[2,6,8,512]{3,2,1,0:T(8,128)(2,1)S(1)} %get-tuple-element.23), channel_id=1, source_target_pairs={{0,2},{1,3},{2,4},{3,5},{4,6},{5,7},{6,8},{7,9},{8,10},{9,11},{10,... | collective-permute-start | bytes 294920 | tf_op jit(solution)/shard_map/ppermute | solution.py:371
  43.8 1.9 %collective-permute-start.4 = (bf16[2,6,8,512]{3,2,1,0:T(8,128)(2,1)S(1)}, bf16[2,6,8,512]{3,2,1,0:T(8,128)(2,1)S(1)}, u32[]{:S(2)}, u32[]{:S(2)}) collective-permute-start(bf16[2,6,8,512]{3,2,1,0:T(8,128)(2,1)S(1)} %get-tuple-element.24), channel_id=1, source_target_pairs={{2,0},{3,1},{4,2},{5,3},{6,4},{7,5},{8,6},{9,7},{10,8},{11,9},{12,... | collective-permute-start | bytes 294920 | tf_op jit(solution)/shard_map/ppermute | solution.py:371
  45.7 0.0 collective-permute-done.3.above_corner
  45.8 5.5 %collective-permute-done.4.below_corner = bf16[2,6,8,512]{3,2,1,0:T(8,128)(2,1)S(1)} collective-permute-done((bf16[2,6,8,512]{3,2,1,0:T(8,128)(2,1)S(1)}, bf16[2,6,8,512]{3,2,1,0:T(8,128)(2,1)S(1)}, u32[]{:S(2)}, u32[]{:S(2)}) %collective-permute-start.4) | collective-permute-done | bytes 98336 | tf_op jit(solution)/shard_map/ppermute | solution.py:371
  51.3 0.0 collective-permute-done.above
  51.3 0.0 collective-permute-done.1.below
  51.3 0.0 copy-done.2
  51.3 8.7 %crossing.1 = (bf16[16,64,512]{2,1,0:T(8,128)(2,1)S(1)}, f32[8,128]{1,0:T(8,128)S(1)}) custom-call(f32[16,64,512]{2,1,0:T(8,128)} %bitcast.15, f32[16,64,512]{2,1,0:T(8,128)} %bitcast.24, bf16[2,8,64,512]{3,2,1,0:T(8,128)(2,1)S(1)} %collective-permute-done.above, bf16[2,8,64,512]{3,2,1,0:T(8,128)(2,1)S(1)} %collective-permute-done.1.below, ...), custom_call_target="tpu_custom_call" | custom-call | flops 50000000 | bytes 6291456 | tf_op jit(solution)/shard_map/crossing/pallas_call | solution.py:201
  60.0 6.0 %collective-permute-start.5 = (bf16[16,64,512]{2,1,0:T(8,128)(2,1)S(1)}, bf16[16,64,512]{2,1,0:T(8,128)(2,1)S(1)}, u32[]{:S(2)}, u32[]{:S(2)}) collective-permute-start(bf16[16,64,512]{2,1,0:T(8,128)(2,1)S(1)} %get-tuple-element.26), channel_id=1, source_target_pairs={{16,32},{17,33},{18,34},{19,35},{20,36},{21,37},{22,38},{23,39},{2... | collective-permute-start | bytes 3145736 | tf_op jit(solution)/shard_map/ppermute | solution.py:371
  66.0 8.7 %staying.1 = (bf16[16,64,512]{2,1,0:T(8,128)(2,1)S(1)}, f32[8,128]{1,0:T(8,128)S(1)}) custom-call(f32[16,64,512]{2,1,0:T(8,128)} %bitcast.16, f32[16,64,512]{2,1,0:T(8,128)} %bitcast.25, bf16[2,8,64,512]{3,2,1,0:T(8,128)(2,1)S(1)} %collective-permute-done.above, bf16[2,8,64,512]{3,2,1,0:T(8,128)(2,1)S(1)} %collective-permute-done.1.below, ...), custom_call_target="tpu_custom_call" | custom-call | flops 50000000 | bytes 6291456 | tf_op jit(solution)/shard_map/staying/pallas_call | solution.py:201
  74.6 0.1 collective-permute-start.6
  74.7 0.0 copy-start.1
  74.7 4.0 %spread.1 = bf16[2048,512]{1,0:T(8,128)(2,1)} custom-call(s32[1]{0:T(128)} %bitcast.1.count, s32[1,2048]{1,0:T(1,128)S(1)} %bitcast.20, bf16[1024,512]{1,0:T(8,128)(2,1)S(1)} %get-tuple-element.31.tangents, f32[8,128]{1,0:T(8,128)S(1)} %get-tuple-element.32._), custom_call_target="tpu_custom_call" | custom-call | flops 2147483648 | bytes 4194304 | tf_op jit(solution)/shard_map/spread/pallas_call | solution.py:346
  78.8 0.0 collective-permute-done.5.from_chip
  78.8 0.0 collective-permute-done.6.from_core
  78.8 0.0 copy-done.1
  78.8 2.6 %final.1 = (f32[16,64,512]{2,1,0:T(8,128)}, f32[16,64,512]{2,1,0:T(8,128)}) custom-call(f32[16,64,512]{2,1,0:T(8,128)S(1)} %bitcast.17, f32[16,64,512]{2,1,0:T(8,128)S(1)} %bitcast.18, bf16[16,64,512]{2,1,0:T(8,128)(2,1)S(1)} %collective-permute-done.5.from_chip, bf16[16,64,512]{2,1,0:T(8,128)(2,1)S(1)} %collective-permute-done.6.from_core), custom_call_target="tpu_custom_call" | custom-call | flops 4000000 | bytes 10485760 | tf_op jit(solution)/shard_map/final/pallas_call | solution.py:231
  (1 shorter events, 0.0 us)
Async XLA Ops:
  0.6 11.6 %copy-start = (s32[1,16]{1,0:T(1,128)S(1)}, s32[1,16]{1,0:T(1,128)}, u32[]{:S(2)}) copy-start(s32[1,16]{1,0:T(1,128)} %param.15) | copy-start | bytes 196
  0.6 12.2 %copy-start.3 = (s32[1,1,2048]{2,1,0:T(1,128)S(1)}, s32[1,1,2048]{2,1,0:T(1,128)}, u32[]{:S(2)}) copy-start(s32[1,1,2048]{2,1,0:T(1,128)} %param.14) | copy-start | bytes 24580
  0.7 12.2 %copy-start.4 = (f32[1024]{0:T(1024)S(1)}, f32[1024]{0:T(1024)}, u32[]{:S(2)}) copy-start(f32[1024]{0:T(1024)} %param.18) | copy-start | bytes 12292
  4.0 47.3 %collective-permute-start = (bf16[2,8,64,512]{3,2,1,0:T(8,128)(2,1)}, bf16[2,8,64,512]{3,2,1,0:T(8,128)(2,1)S(1)}, u32[]{:S(2)}, u32[]{:S(2)}) collective-permute-start(bf16[2,8,64,512]{3,2,1,0:T(8,128)(2,1)} %get-tuple-element.19), channel_id=1, source_target_pairs={{0,2},{1,3},{2,4},{3,5},{4,6},{5,7},{6,8},{7,9},{8,10},{9,11},{10,... | collective-permute-start | bytes 3145736 | tf_op jit(solution)/shard_map/ppermute | solution.py:371
  5.9 45.4 %collective-permute-start.1 = (bf16[2,8,64,512]{3,2,1,0:T(8,128)(2,1)S(1)}, bf16[2,8,64,512]{3,2,1,0:T(8,128)(2,1)S(1)}, u32[]{:S(2)}, u32[]{:S(2)}) collective-permute-start(bf16[2,8,64,512]{3,2,1,0:T(8,128)(2,1)S(1)} %get-tuple-element.20), channel_id=1, source_target_pairs={{2,0},{3,1},{4,2},{5,3},{6,4},{7,5},{8,6},{9,7},{10,8},{11,9},{12,... | collective-permute-start | bytes 3145736 | tf_op jit(solution)/shard_map/ppermute | solution.py:371
  9.3 28.2 %collective-permute-start.2 = (bf16[2,16,8,512]{3,2,1,0:T(8,128)(2,1)}, bf16[2,16,8,512]{3,2,1,0:T(8,128)(2,1)S(1)}, u32[]{:S(2)}, u32[]{:S(2)}) collective-permute-start(bf16[2,16,8,512]{3,2,1,0:T(8,128)(2,1)} %get-tuple-element.21), channel_id=1, source_target_pairs={{0,1},{1,0},{2,3},{3,2},{4,5},{5,4},{6,7},{7,6},{8,9},{9,8},{10,11... | collective-permute-start | bytes 786440 | tf_op jit(solution)/shard_map/ppermute | solution.py:371
  12.9 38.4 %copy-start.2 = (f32[8,512]{1,0:T(8,128)S(1)}, f32[8,512]{1,0:T(8,128)}, u32[]{:S(2)}) copy-start(f32[8,512]{1,0:T(8,128)} %rates.3) | copy-start | bytes 49156
  37.5 8.2 %collective-permute-start.3 = (bf16[2,6,8,512]{3,2,1,0:T(8,128)(2,1)S(1)}, bf16[2,6,8,512]{3,2,1,0:T(8,128)(2,1)S(1)}, u32[]{:S(2)}, u32[]{:S(2)}) collective-permute-start(bf16[2,6,8,512]{3,2,1,0:T(8,128)(2,1)S(1)} %get-tuple-element.23), channel_id=1, source_target_pairs={{0,2},{1,3},{2,4},{3,5},{4,6},{5,7},{6,8},{7,9},{8,10},{9,11},{10,... | collective-permute-start | bytes 294920 | tf_op jit(solution)/shard_map/ppermute | solution.py:371
  43.8 7.5 %collective-permute-start.4 = (bf16[2,6,8,512]{3,2,1,0:T(8,128)(2,1)S(1)}, bf16[2,6,8,512]{3,2,1,0:T(8,128)(2,1)S(1)}, u32[]{:S(2)}, u32[]{:S(2)}) collective-permute-start(bf16[2,6,8,512]{3,2,1,0:T(8,128)(2,1)S(1)} %get-tuple-element.24), channel_id=1, source_target_pairs={{2,0},{3,1},{4,2},{5,3},{6,4},{7,5},{8,6},{9,7},{10,8},{11,9},{12,... | collective-permute-start | bytes 294920 | tf_op jit(solution)/shard_map/ppermute | solution.py:371
  60.0 18.8 %collective-permute-start.5 = (bf16[16,64,512]{2,1,0:T(8,128)(2,1)S(1)}, bf16[16,64,512]{2,1,0:T(8,128)(2,1)S(1)}, u32[]{:S(2)}, u32[]{:S(2)}) collective-permute-start(bf16[16,64,512]{2,1,0:T(8,128)(2,1)S(1)} %get-tuple-element.26), channel_id=1, source_target_pairs={{16,32},{17,33},{18,34},{19,35},{20,36},{21,37},{22,38},{23,39},{2... | collective-permute-start | bytes 3145736 | tf_op jit(solution)/shard_map/ppermute | solution.py:371
  74.6 4.1 %collective-permute-start.6 = (bf16[16,64,512]{2,1,0:T(8,128)(2,1)S(1)}, bf16[16,64,512]{2,1,0:T(8,128)(2,1)S(1)}, u32[]{:S(2)}, u32[]{:S(2)}) collective-permute-start(bf16[16,64,512]{2,1,0:T(8,128)(2,1)S(1)} %get-tuple-element.28), channel_id=1, source_target_pairs={{0,16},{1,17},{2,18},{3,19},{4,20},{5,21},{6,22},{7,23},{8,24},{9,... | collective-permute-start | bytes 3145736 | tf_op jit(solution)/shard_map/ppermute | solution.py:371
  74.7 4.1 %copy-start.1 = (f32[1,16,64,512]{3,2,1,0:T(8,128)S(1)}, f32[1,16,64,512]{3,2,1,0:T(8,128)}, u32[]{:S(2)}) copy-start(f32[1,16,64,512]{3,2,1,0:T(8,128)} %param.10) | copy-start | bytes 6291460

commit v2 on v1

--- a/solution.py
+++ b/solution.py
@@ -14,6 +14,7 @@
 LANES = 128
 COLS_TILE = 256
 SLOTS_TILE = 512
+PARTS = 2
 MIRROR = (3, 2, 1, 0, 7, 6, 5, 4)
 TOKEN = jax.ShapeDtypeStruct((8, LANES), jnp.float32)
 
@@ -85,9 +86,7 @@
 def sweep(src, dst, taps, first, last, blocks):
     c0, c1, c2, c3, c4, c5, c6, c7 = taps
     group = 4
-
-    def rows_of(it, carry):
-        i = first + it * group
+    for i in range(first, last, group):
         for b in range(blocks):
             j = 8 + 8 * b
             at = [src[i - 2 + r, j : j + 8, :] for r in range(group + 4)]
@@ -101,21 +100,18 @@
                 total = total + c6 * src[i + r, j + 1 : j + 9, :]
                 total = total + c7 * src[i + r, j + 2 : j + 10, :]
                 dst[i + r, j : j + 8, :] = total
-        return carry
-
-    lax.fori_loop(0, (last - first) // group, rows_of, 0)
 
 
 def transport_kernel(
-    crossing, inc, mul, above, below, strip, above_corner, below_corner, rates, _, out, token, bufs, other, sems
+    crossing, low_tile, inc, mul, above, below, strip, above_corner, below_corner, rates, _, out, token, bufs, other, sems
 ):
     lat, lon = lax.axis_index("lat"), lax.axis_index("lon")
     odd = lax.rem(lax.axis_index("sub"), 2)
     n_lat = lax.axis_size("lat")
-    rows, across, levels = inc.shape
+    rows, across = inc.shape[0], inc.shape[1]
     tall = rows + 2 * REACH
     blocks = (across + REACH) // 8
-    tiles = levels // LANES
+    tiles = bufs.shape[0]
     own = pl.multiple_of(8 + REACH * lon, 8)
     beside = pl.multiple_of(8 + across * (1 - lon), 8)
     f = 1 - odd if crossing else odd
@@ -123,7 +119,7 @@
 
     def arriving(src, t):
         there = bufs.at[t, pl.ds(REACH, rows), pl.ds(own, across), :]
-        return pltpu.make_async_copy(src.at[:, :, pl.ds(t * LANES, LANES)], there, sems.at[t])
+        return pltpu.make_async_copy(src.at[:, :, pl.ds((low_tile + t) * LANES, LANES)], there, sems.at[t])
 
     @pl.when(forward)
     def _():
@@ -146,7 +142,7 @@
         for r in (0, 1, tall - 2, tall - 1):
             bufs[t, r, pl.ds(beside, REACH), :] = blank
         for r in range(REACH):
-            lanes = slice(t * LANES, (t + 1) * LANES)
+            lanes = slice((low_tile + t) * LANES, (low_tile + t + 1) * LANES)
             bufs[t, r, pl.ds(own, across), :] = above[f, r, :, lanes].astype(jnp.float32)
             bufs[t, rows + REACH + r, pl.ds(own, across), :] = below[f, r, :, lanes].astype(jnp.float32)
         for r in range(rows):
@@ -156,7 +152,8 @@
             bufs[t, rows + REACH + r, pl.ds(beside, REACH), :] = below_corner[f, r, :, lanes].astype(jnp.float32)
 
     def tile_of(t, carry):
-        lanes = pl.ds(pl.multiple_of(t * LANES, LANES), LANES)
+        lanes = pl.ds(pl.multiple_of((low_tile + t) * LANES, LANES), LANES)
+        out_lanes = pl.ds(pl.multiple_of(t * LANES, LANES), LANES)
         pltpu.make_async_copy(
             inc.at[:, :, lanes], bufs.at[t, pl.ds(REACH, rows), pl.ds(own, across), :], sems.at[t]
         ).wait()
@@ -188,56 +185,61 @@
 
             a, b = b, a
         for r in range(rows):
-            out[r, :, lanes] = (scale[0:1] * a[REACH + r, pl.ds(own, across), :]).astype(jnp.bfloat16)
+            out[r, :, out_lanes] = (scale[0:1] * a[REACH + r, pl.ds(own, across), :]).astype(jnp.bfloat16)
         return carry
 
     lax.fori_loop(0, tiles, tile_of, 0)
 
 
-def transported(crossing, increment, multiplier, pieces, rates, token):
-    rows, across, levels = increment.shape
-    tall, wide, tiles = rows + 2 * REACH, across + REACH + 16, levels // LANES
+def transported(crossing, low_tile, tiles, increment, multiplier, pieces, rates, token):
+    rows, across, _ = increment.shape
+    tall, wide = rows + 2 * REACH, across + REACH + 16
     hbm, vmem = pl.BlockSpec(memory_space=pltpu.HBM), pl.BlockSpec(memory_space=pltpu.VMEM)
     return pl.pallas_call(
-        functools.partial(transport_kernel, crossing),
+        functools.partial(transport_kernel, crossing, low_tile),
         in_specs=[hbm, hbm] + [vmem] * (len(pieces) + 1) + [pl.BlockSpec(memory_space=pl.ANY)],
         out_specs=[vmem, vmem],
-        out_shape=[jax.ShapeDtypeStruct(increment.shape, jnp.bfloat16), TOKEN],
+        out_shape=[jax.ShapeDtypeStruct((rows, across, tiles * LANES), jnp.bfloat16), TOKEN],
         scratch_shapes=[
             pltpu.VMEM((tiles, tall, wide, LANES), jnp.float32),
             pltpu.VMEM((tall, wide, LANES), jnp.float32),
             pltpu.SemaphoreType.DMA((tiles,)),
         ],
         compiler_params=pltpu.CompilerParams(vmem_limit_bytes=24 << 20),
-        cost_estimate=pl.CostEstimate(flops=50_000_000, bytes_accessed=6 << 20, transcendentals=0),
+        cost_estimate=pl.CostEstimate(flops=12_500_000 * tiles, bytes_accessed=tiles << 20, transcendentals=0),
         name="crossing" if crossing else "staying",
     )(*in_hbm(increment, multiplier), *pieces, rates, token)
 
 
-def final_kernel(inc, base, from_chip, from_core, error_out, grad_out):
+def final_kernel(inc, base, from_core, *refs):
     odd = lax.rem(lax.axis_index("sub"), 2) == 1
+    from_chip, (error_out, grad_out) = refs[:-2], refs[-2:]
+    width = from_chip[0].shape[2]
     group = 2
     for r in range(0, inc.shape[0], group):
         rows = slice(r, r + group)
-        x = from_chip[rows].astype(jnp.float32)
-        d = from_core[rows].astype(jnp.float32)
-        error_out[rows] = inc[rows] - jnp.where(odd, d, x)
-        grad_out[rows] = base[rows] - jnp.where(odd, x, d)
-
-
-def final(increment, base, from_chip, from_core):
+        for part, ref in enumerate(from_chip):
+            lanes = slice(part * width, (part + 1) * width)
+            x = ref[rows].astype(jnp.float32)
+            d = from_core[rows, :, lanes].astype(jnp.float32)
+            error_out[rows, :, lanes] = inc[rows, :, lanes] - jnp.where(odd, d, x)
+            grad_out[rows, :, lanes] = base[rows, :, lanes] - jnp.where(odd, x, d)
+
+
+def final(increment, base, from_core, from_chip):
     rows, across, levels = increment.shape
     block = pl.BlockSpec((4, across, levels), lambda i: (i, 0, 0))
+    part = pl.BlockSpec((4, across, levels // len(from_chip)), lambda i: (i, 0, 0))
     return pl.pallas_call(
         final_kernel,
         grid=(rows // 4,),
-        in_specs=[block] * 4,
+        in_specs=[block] * 3 + [part] * len(from_chip),
         out_specs=[block] * 2,
         out_shape=[jax.ShapeDtypeStruct(increment.shape, jnp.float32)] * 2,
         compiler_params=pltpu.CompilerParams(vmem_limit_bytes=16 << 20),
         cost_estimate=pl.CostEstimate(flops=4_000_000, bytes_accessed=10 << 20, transcendentals=0),
         name="final",
-    )(increment, base, from_chip, from_core)
+    )(increment, base, from_core, *from_chip)
 
 
 ROWS_BY_COLS = (((1,), (1,)), ((), ()))
@@ -319,8 +321,9 @@
     )(count, columns, hidden_bias, *in_hbm(*moved))
 
 
-def spread_kernel(count, columns, tangents, _, out, held, sems):
+def spread_kernel(count, columns, tangents, _, out, token, held, sems):
     slots, cols = held.shape[0], tangents.shape[0]
+    token[...] = jnp.zeros_like(token)
     lane = lax.broadcasted_iota(jnp.int32, (LANES, LANES), 1)
     outs = []
     for i, start in enumerate(range(0, slots, SLOTS_TILE)):
@@ -346,8 +349,8 @@
     return pl.pallas_call(
         spread_kernel,
         in_specs=[pl.BlockSpec(memory_space=pltpu.SMEM), vmem, vmem, pl.BlockSpec(memory_space=pl.ANY)],
-        out_specs=pl.BlockSpec(memory_space=pltpu.HBM),
-        out_shape=jax.ShapeDtypeStruct((slots, chan), jnp.bfloat16),
+        out_specs=[pl.BlockSpec(memory_space=pltpu.HBM), vmem],
+        out_shape=[jax.ShapeDtypeStruct((slots, chan), jnp.bfloat16), TOKEN],
         scratch_shapes=[
             pltpu.VMEM((slots, chan), jnp.bfloat16),
             pltpu.SemaphoreType.DMA((slots // SLOTS_TILE,)),
@@ -406,12 +409,17 @@
     above_corner = sent(high_corner, lambda s, a, o: (s, a + 1, o))
     below_corner = sent(low_corner, lambda s, a, o: (s, a - 1, o))
     pieces = [above, below, across, above_corner, below_corner]
-    crossing, token = transported(True, increment, multiplier, pieces, transport, token)
-    from_chip = sent(crossing, lambda s, a, o: (s + 1 if s % 2 else s - 1, a, o))
-    staying, token = transported(False, increment, multiplier, pieces, transport, token)
+    tangent, token = spread(my_count, obs_column[0], tangents, token)
+    tiles = levels // LANES
+    from_chip = []
+    for part in range(PARTS):
+        crossing, token = transported(
+            True, part * tiles // PARTS, tiles // PARTS, increment, multiplier, pieces, transport, token
+        )
+        from_chip.append(sent(crossing, lambda s, a, o: (s + 1 if s % 2 else s - 1, a, o)))
+    staying, _ = transported(False, 0, tiles, increment, multiplier, pieces, transport, token)
     from_core = sent(staying, lambda s, a, o: (s - 1 if s % 2 else s + 1, a, o))
-    tangent = spread(my_count, obs_column[0], tangents, token)
-    model_error, gradient = final(increment, base.reshape(increment.shape), from_chip, from_core)
+    model_error, gradient = final(increment, base.reshape(increment.shape), from_core, from_chip)
     return (model_error[None], gradient[None], tangent[None, None])
 
 

time: 81.7 us -> 92.4 us (1.13)
  the two profiles are of different devices: /device:TPU:97 before, /device:TPU:13 now
where the time goes in v2:
time: 92.4 us; the launch traced here: 92.1 us
  Pallas kernels  39.5 us (43%)
  waiting for transfers between devices  26.1 us (28%)
  starting transfers between devices  25.2 us (27%)
    ppermute x8, waiting for transfers between devices, sent(): return lax.ppermute(array, ('sub', 'lat', 'lon'), pairs)  26.1 us
    ppermute x8, starting transfers between devices, sent(): return lax.ppermute(array, ('sub', 'lat', 'lon'), pairs)  25.2 us
    pallas_call x3, Pallas kernels, transported(): pl.pallas_call(functools.partial(transport_kernel, crossing, low_tile), i...  17.8 us
    pallas_call x1, Pallas kernels, network(): pl.pallas_call(network_kernel, in_specs=[pl.BlockSpec(memory_space=pltpu....  12 us
    pallas_call x1, Pallas kernels, spread(): pl.pallas_call(spread_kernel, in_specs=[pl.BlockSpec(memory_space=pltpu.S...  3.79 us
    pallas_call x1, Pallas kernels, pack(): pl.pallas_call(pack_kernel, in_specs=[pl.BlockSpec(memory_space=pltpu.HBM...  3.31 us
    pallas_call x1, Pallas kernels, final(): pl.pallas_call(final_kernel, grid=(rows // 4,), in_specs=[block] * 3 + [p...  2.56 us
  transfers between devices with their start and end apart: 8, of which 3 were waited for; matrix products, arithmetic and copies ran while one was open for 1% of the time, Pallas kernels for 17%

profile of v2, /device:TPU:13, one launch (start us, length us, event | category | flops | bytes accessed | tf_op | source)
XLA Modules:
  0.0 92.1 jit_solution(16017363595248004651)
XLA Ops:
  0.6 0.0 copy-start
  0.6 0.0 copy-start.3
  0.7 0.0 copy-start.4
  0.7 3.3 %pack.1 = (bf16[2,8,64,512]{3,2,1,0:T(8,128)(2,1)S(1)}, bf16[2,8,64,512]{3,2,1,0:T(8,128)(2,1)}, bf16[2,16,8,512]{3,2,1,0:T(8,128)(2,1)}) custom-call(f32[16,64,512]{2,1,0:T(8,128)} %bitcast.13, f32[16,64,512]{2,1,0:T(8,128)} %bitcast.23), custom_call_target="tpu_custom_call" | custom-call | tf_op jit(solution)/shard_map/pack/pallas_call | solution.py:54
  4.0 3.5 %collective-permute-start = (bf16[2,8,64,512]{3,2,1,0:T(8,128)(2,1)}, bf16[2,8,64,512]{3,2,1,0:T(8,128)(2,1)S(1)}, u32[]{:S(2)}, u32[]{:S(2)}) collective-permute-start(bf16[2,8,64,512]{3,2,1,0:T(8,128)(2,1)} %get-tuple-element.22), channel_id=1, source_target_pairs={{0,2},{1,3},{2,4},{3,5},{4,6},{5,7},{6,8},{7,9},{8,10},{9,11},{10,... | collective-permute-start | bytes 3145736 | tf_op jit(solution)/shard_map/ppermute | solution.py:374
  7.5 3.9 %collective-permute-start.1 = (bf16[2,8,64,512]{3,2,1,0:T(8,128)(2,1)S(1)}, bf16[2,8,64,512]{3,2,1,0:T(8,128)(2,1)S(1)}, u32[]{:S(2)}, u32[]{:S(2)}) collective-permute-start(bf16[2,8,64,512]{3,2,1,0:T(8,128)(2,1)S(1)} %get-tuple-element.23), channel_id=1, source_target_pairs={{2,0},{3,1},{4,2},{5,3},{6,4},{7,5},{8,6},{9,7},{10,8},{11,9},{12,... | collective-permute-start | bytes 3145736 | tf_op jit(solution)/shard_map/ppermute | solution.py:374
  11.5 2.4 %collective-permute-start.2 = (bf16[2,16,8,512]{3,2,1,0:T(8,128)(2,1)}, bf16[2,16,8,512]{3,2,1,0:T(8,128)(2,1)S(1)}, u32[]{:S(2)}, u32[]{:S(2)}) collective-permute-start(bf16[2,16,8,512]{3,2,1,0:T(8,128)(2,1)} %get-tuple-element.24), channel_id=1, source_target_pairs={{0,1},{1,0},{2,3},{3,2},{4,5},{5,4},{6,7},{7,6},{8,9},{9,8},{10,11... | collective-permute-start | bytes 786440 | tf_op jit(solution)/shard_map/ppermute | solution.py:374
  13.9 0.0 copy-done
  13.9 0.6 constant_dynamic-slice_fusion
  14.4 0.0 copy-done.3
  14.4 12.0 %network.1 = (bf16[1024,512]{1,0:T(8,128)(2,1)S(1)}, f32[1024,512]{1,0:T(8,128)S(1)}, f32[8,128]{1,0:T(8,128)S(1)}) custom-call(s32[1]{0:T(128)} %bitcast.1.count, s32[1,2048]{1,0:T(1,128)S(1)} %bitcast.20, f32[1,1024]{1,0:T(1,128)S(1)} %bitcast.22, f32[1024,512]{1,0:T(8,128)} %bitcast.14, bf16[1024,512]{1,0:T(8,128)(2,1)} %bitcast.31, ...), custom_call_target="tpu_custom_call" | custom-call | flops 7516192768 | bytes 12582912 | tf_op jit(solution)/shard_map/network/pallas_call | solution.py:303
  26.4 15.5 %collective-permute-done.2.strip = bf16[2,16,8,512]{3,2,1,0:T(8,128)(2,1)S(1)} collective-permute-done((bf16[2,16,8,512]{3,2,1,0:T(8,128)(2,1)}, bf16[2,16,8,512]{3,2,1,0:T(8,128)(2,1)S(1)}, u32[]{:S(2)}, u32[]{:S(2)}) %collective-permute-start.2) | collective-permute-done | bytes 262176 | tf_op jit(solution)/shard_map/ppermute | solution.py:374
  42.0 1.9 %collective-permute-start.3 = (bf16[2,6,8,512]{3,2,1,0:T(8,128)(2,1)S(1)}, bf16[2,6,8,512]{3,2,1,0:T(8,128)(2,1)S(1)}, u32[]{:S(2)}, u32[]{:S(2)}) collective-permute-start(bf16[2,6,8,512]{3,2,1,0:T(8,128)(2,1)S(1)} %get-tuple-element.26), channel_id=1, source_target_pairs={{0,2},{1,3},{2,4},{3,5},{4,6},{5,7},{6,8},{7,9},{8,10},{9,11},{10,... | collective-permute-start | bytes 294920 | tf_op jit(solution)/shard_map/ppermute | solution.py:374
  43.9 5.7 %collective-permute-start.4 = (bf16[2,6,8,512]{3,2,1,0:T(8,128)(2,1)S(1)}, bf16[2,6,8,512]{3,2,1,0:T(8,128)(2,1)S(1)}, u32[]{:S(2)}, u32[]{:S(2)}) collective-permute-start(bf16[2,6,8,512]{3,2,1,0:T(8,128)(2,1)S(1)} %get-tuple-element.27), channel_id=1, source_target_pairs={{2,0},{3,1},{4,2},{5,3},{6,4},{7,5},{8,6},{9,7},{10,8},{11,9},{12,... | collective-permute-start | bytes 294920 | tf_op jit(solution)/shard_map/ppermute | solution.py:374
  49.6 0.0 copy-start.2
  49.6 3.8 %spread.1 = (bf16[2048,512]{1,0:T(8,128)(2,1)}, f32[8,128]{1,0:T(8,128)S(1)}) custom-call(s32[1]{0:T(128)} %bitcast.1.count, s32[1,2048]{1,0:T(1,128)S(1)} %bitcast.21, bf16[1024,512]{1,0:T(8,128)(2,1)S(1)} %get-tuple-element.28.tangents, f32[8,128]{1,0:T(8,128)S(1)} %get-tuple-element.29._), custom_call_target="tpu_custom_call" | custom-call | flops 2147483648 | bytes 4194304 | tf_op jit(solution)/shard_map/spread/pallas_call | solution.py:349
  53.4 0.0 collective-permute-done.3.above_corner
  53.4 0.0 collective-permute-done.4.below_corner
  53.4 0.0 collective-permute-done.above
  53.4 0.0 collective-permute-done.1.below
  53.4 4.6 %crossing.2 = (bf16[16,64,256]{2,1,0:T(8,128)(2,1)S(1)}, f32[8,128]{1,0:T(8,128)S(1)}) custom-call(f32[16,64,512]{2,1,0:T(8,128)} %bitcast.15, f32[16,64,512]{2,1,0:T(8,128)} %bitcast.25, bf16[2,8,64,512]{3,2,1,0:T(8,128)(2,1)S(1)} %collective-permute-done.above, bf16[2,8,64,512]{3,2,1,0:T(8,128)(2,1)S(1)} %collective-permute-done.1.below, ...), custom_call_target="tpu_custom_call" | custom-call | flops 25000000 | bytes 2097152 | tf_op jit(solution)/shard_map/crossing/pallas_call | solution.py:198
  58.0 4.6 %crossing.3 = (bf16[16,64,256]{2,1,0:T(8,128)(2,1)S(1)}, f32[8,128]{1,0:T(8,128)S(1)}) custom-call(f32[16,64,512]{2,1,0:T(8,128)} %bitcast.16, f32[16,64,512]{2,1,0:T(8,128)} %bitcast.26, bf16[2,8,64,512]{3,2,1,0:T(8,128)(2,1)S(1)} %collective-permute-done.above, bf16[2,8,64,512]{3,2,1,0:T(8,128)(2,1)S(1)} %collective-permute-done.1.below, ...), custom_call_target="tpu_custom_call" | custom-call | flops 25000000 | bytes 2097152 | tf_op jit(solution)/shard_map/crossing/pallas_call | solution.py:198
  62.7 0.0 copy-start.1
  62.7 8.6 %staying.1 = (bf16[16,64,512]{2,1,0:T(8,128)(2,1)S(1)}, f32[8,128]{1,0:T(8,128)}) custom-call(f32[16,64,512]{2,1,0:T(8,128)} %bitcast.17, f32[16,64,512]{2,1,0:T(8,128)} %bitcast.27, bf16[2,8,64,512]{3,2,1,0:T(8,128)(2,1)S(1)} %collective-permute-done.above, bf16[2,8,64,512]{3,2,1,0:T(8,128)(2,1)S(1)} %collective-permute-done.1.below, ...), custom_call_target="tpu_custom_call" | custom-call | flops 50000000 | bytes 4194304 | tf_op jit(solution)/shard_map/staying/pallas_call | solution.py:198
  71.3 2.2 %collective-permute-start.5 = (bf16[16,64,512]{2,1,0:T(8,128)(2,1)S(1)}, bf16[16,64,512]{2,1,0:T(8,128)(2,1)S(1)}, u32[]{:S(2)}, u32[]{:S(2)}) collective-permute-start(bf16[16,64,512]{2,1,0:T(8,128)(2,1)S(1)} %get-tuple-element.33), channel_id=1, source_target_pairs={{0,16},{1,17},{2,18},{3,19},{4,20},{5,21},{6,22},{7,23},{8,24},{9,... | collective-permute-start | bytes 3145736 | tf_op jit(solution)/shard_map/ppermute | solution.py:374
  73.4 2.7 %collective-permute-start.7 = (bf16[16,64,256]{2,1,0:T(8,128)(2,1)S(1)}, bf16[16,64,256]{2,1,0:T(8,128)(2,1)S(1)}, u32[]{:S(2)}, u32[]{:S(2)}) collective-permute-start(bf16[16,64,256]{2,1,0:T(8,128)(2,1)S(1)} %get-tuple-element.35), channel_id=1, source_target_pairs={{16,32},{17,33},{18,34},{19,35},{20,36},{21,37},{22,38},{23,39},{2... | collective-permute-start | bytes 1572872 | tf_op jit(solution)/shard_map/ppermute | solution.py:374
  76.2 2.8 %collective-permute-start.6 = (bf16[16,64,256]{2,1,0:T(8,128)(2,1)S(1)}, bf16[16,64,256]{2,1,0:T(8,128)(2,1)S(1)}, u32[]{:S(2)}, u32[]{:S(2)}) collective-permute-start(bf16[16,64,256]{2,1,0:T(8,128)(2,1)S(1)} %get-tuple-element.34), channel_id=1, source_target_pairs={{16,32},{17,33},{18,34},{19,35},{20,36},{21,37},{22,38},{23,39},{2... | collective-permute-start | bytes 1572872 | tf_op jit(solution)/shard_map/ppermute | solution.py:374
  79.0 5.2 %collective-permute-done.7.refs_1_ = bf16[16,64,256]{2,1,0:T(8,128)(2,1)S(1)} collective-permute-done((bf16[16,64,256]{2,1,0:T(8,128)(2,1)S(1)}, bf16[16,64,256]{2,1,0:T(8,128)(2,1)S(1)}, u32[]{:S(2)}, u32[]{:S(2)}) %collective-permute-start.7) | collective-permute-done | bytes 524320 | tf_op jit(solution)/shard_map/ppermute | solution.py:374
  84.2 5.3 %collective-permute-done.6.refs_0_ = bf16[16,64,256]{2,1,0:T(8,128)(2,1)S(1)} collective-permute-done((bf16[16,64,256]{2,1,0:T(8,128)(2,1)S(1)}, bf16[16,64,256]{2,1,0:T(8,128)(2,1)S(1)}, u32[]{:S(2)}, u32[]{:S(2)}) %collective-permute-start.6) | collective-permute-done | bytes 524320 | tf_op jit(solution)/shard_map/ppermute | solution.py:374
  89.5 0.0 collective-permute-done.5.from_core
  89.5 0.0 copy-done.1
  89.5 2.6 %final.1 = (f32[16,64,512]{2,1,0:T(8,128)}, f32[16,64,512]{2,1,0:T(8,128)}) custom-call(f32[16,64,512]{2,1,0:T(8,128)S(1)} %bitcast.18, f32[16,64,512]{2,1,0:T(8,128)S(1)} %bitcast.19, bf16[16,64,512]{2,1,0:T(8,128)(2,1)S(1)} %collective-permute-done.5.from_core, bf16[16,64,256]{2,1,0:T(8,128)(2,1)S(1)} %collective-permute-done.6.refs_0_, ...), custom_call_target="tpu_custom_call" | custom-call | flops 4000000 | bytes 10485760 | tf_op jit(solution)/shard_map/final/pallas_call | solution.py:233
  (3 shorter events, 0.0 us)
Async XLA Ops:
  0.6 13.2 %copy-start = (s32[1,16]{1,0:T(1,128)S(1)}, s32[1,16]{1,0:T(1,128)}, u32[]{:S(2)}) copy-start(s32[1,16]{1,0:T(1,128)} %param.15) | copy-start | bytes 196
  0.6 13.8 %copy-start.3 = (s32[1,1,2048]{2,1,0:T(1,128)S(1)}, s32[1,1,2048]{2,1,0:T(1,128)}, u32[]{:S(2)}) copy-start(s32[1,1,2048]{2,1,0:T(1,128)} %param.14) | copy-start | bytes 24580
  0.7 13.8 %copy-start.4 = (f32[1024]{0:T(1024)S(1)}, f32[1024]{0:T(1024)}, u32[]{:S(2)}) copy-start(f32[1024]{0:T(1024)} %param.18) | copy-start | bytes 12292
  4.0 49.4 %collective-permute-start = (bf16[2,8,64,512]{3,2,1,0:T(8,128)(2,1)}, bf16[2,8,64,512]{3,2,1,0:T(8,128)(2,1)S(1)}, u32[]{:S(2)}, u32[]{:S(2)}) collective-permute-start(bf16[2,8,64,512]{3,2,1,0:T(8,128)(2,1)} %get-tuple-element.22), channel_id=1, source_target_pairs={{0,2},{1,3},{2,4},{3,5},{4,6},{5,7},{6,8},{7,9},{8,10},{9,11},{10,... | collective-permute-start | bytes 3145736 | tf_op jit(solution)/shard_map/ppermute | solution.py:374
  7.5 45.9 %collective-permute-start.1 = (bf16[2,8,64,512]{3,2,1,0:T(8,128)(2,1)S(1)}, bf16[2,8,64,512]{3,2,1,0:T(8,128)(2,1)S(1)}, u32[]{:S(2)}, u32[]{:S(2)}) collective-permute-start(bf16[2,8,64,512]{3,2,1,0:T(8,128)(2,1)S(1)} %get-tuple-element.23), channel_id=1, source_target_pairs={{2,0},{3,1},{4,2},{5,3},{6,4},{7,5},{8,6},{9,7},{10,8},{11,9},{12,... | collective-permute-start | bytes 3145736 | tf_op jit(solution)/shard_map/ppermute | solution.py:374
  11.5 30.5 %collective-permute-start.2 = (bf16[2,16,8,512]{3,2,1,0:T(8,128)(2,1)}, bf16[2,16,8,512]{3,2,1,0:T(8,128)(2,1)S(1)}, u32[]{:S(2)}, u32[]{:S(2)}) collective-permute-start(bf16[2,16,8,512]{3,2,1,0:T(8,128)(2,1)} %get-tuple-element.24), channel_id=1, source_target_pairs={{0,1},{1,0},{2,3},{3,2},{4,5},{5,4},{6,7},{7,6},{8,9},{9,8},{10,11... | collective-permute-start | bytes 786440 | tf_op jit(solution)/shard_map/ppermute | solution.py:374
  42.0 11.4 %collective-permute-start.3 = (bf16[2,6,8,512]{3,2,1,0:T(8,128)(2,1)S(1)}, bf16[2,6,8,512]{3,2,1,0:T(8,128)(2,1)S(1)}, u32[]{:S(2)}, u32[]{:S(2)}) collective-permute-start(bf16[2,6,8,512]{3,2,1,0:T(8,128)(2,1)S(1)} %get-tuple-element.26), channel_id=1, source_target_pairs={{0,2},{1,3},{2,4},{3,5},{4,6},{5,7},{6,8},{7,9},{8,10},{9,11},{10,... | collective-permute-start | bytes 294920 | tf_op jit(solution)/shard_map/ppermute | solution.py:374
  43.9 9.5 %collective-permute-start.4 = (bf16[2,6,8,512]{3,2,1,0:T(8,128)(2,1)S(1)}, bf16[2,6,8,512]{3,2,1,0:T(8,128)(2,1)S(1)}, u32[]{:S(2)}, u32[]{:S(2)}) collective-permute-start(bf16[2,6,8,512]{3,2,1,0:T(8,128)(2,1)S(1)} %get-tuple-element.27), channel_id=1, source_target_pairs={{2,0},{3,1},{4,2},{5,3},{6,4},{7,5},{8,6},{9,7},{10,8},{11,9},{12,... | collective-permute-start | bytes 294920 | tf_op jit(solution)/shard_map/ppermute | solution.py:374
  49.6 3.9 %copy-start.2 = (f32[8,512]{1,0:T(8,128)S(1)}, f32[8,512]{1,0:T(8,128)}, u32[]{:S(2)}) copy-start(f32[8,512]{1,0:T(8,128)} %rates.5) | copy-start | bytes 49156
  62.7 26.9 %copy-start.1 = (f32[1,16,64,512]{3,2,1,0:T(8,128)S(1)}, f32[1,16,64,512]{3,2,1,0:T(8,128)}, u32[]{:S(2)}) copy-start(f32[1,16,64,512]{3,2,1,0:T(8,128)} %param.10) | copy-start | bytes 6291460
  71.3 18.3 %collective-permute-start.5 = (bf16[16,64,512]{2,1,0:T(8,128)(2,1)S(1)}, bf16[16,64,512]{2,1,0:T(8,128)(2,1)S(1)}, u32[]{:S(2)}, u32[]{:S(2)}) collective-permute-start(bf16[16,64,512]{2,1,0:T(8,128)(2,1)S(1)} %get-tuple-element.33), channel_id=1, source_target_pairs={{0,16},{1,17},{2,18},{3,19},{4,20},{5,21},{6,22},{7,23},{8,24},{9,... | collective-permute-start | bytes 3145736 | tf_op jit(solution)/shard_map/ppermute | solution.py:374
  73.4 10.8 %collective-permute-start.7 = (bf16[16,64,256]{2,1,0:T(8,128)(2,1)S(1)}, bf16[16,64,256]{2,1,0:T(8,128)(2,1)S(1)}, u32[]{:S(2)}, u32[]{:S(2)}) collective-permute-start(bf16[16,64,256]{2,1,0:T(8,128)(2,1)S(1)} %get-tuple-element.35), channel_id=1, source_target_pairs={{16,32},{17,33},{18,34},{19,35},{20,36},{21,37},{22,38},{23,39},{2... | collective-permute-start | bytes 1572872 | tf_op jit(solution)/shard_map/ppermute | solution.py:374
  76.2 13.4 %collective-permute-start.6 = (bf16[16,64,256]{2,1,0:T(8,128)(2,1)S(1)}, bf16[16,64,256]{2,1,0:T(8,128)(2,1)S(1)}, u32[]{:S(2)}, u32[]{:S(2)}) collective-permute-start(bf16[16,64,256]{2,1,0:T(8,128)(2,1)S(1)} %get-tuple-element.34), channel_id=1, source_target_pairs={{16,32},{17,33},{18,34},{19,35},{20,36},{21,37},{22,38},{23,39},{2... | collective-permute-start | bytes 1572872 | tf_op jit(solution)/shard_map/ppermute | solution.py:374

commit v3 on v2

--- a/solution.py
+++ b/solution.py
@@ -14,7 +14,6 @@
 LANES = 128
 COLS_TILE = 256
 SLOTS_TILE = 512
-PARTS = 2
 MIRROR = (3, 2, 1, 0, 7, 6, 5, 4)
 TOKEN = jax.ShapeDtypeStruct((8, LANES), jnp.float32)
 
@@ -211,35 +210,36 @@
     )(*in_hbm(increment, multiplier), *pieces, rates, token)
 
 
-def final_kernel(inc, base, from_core, *refs):
+def final_kernel(inc, base, from_chip, from_core, error_out, grad_out, error, grad, sems):
     odd = lax.rem(lax.axis_index("sub"), 2) == 1
-    from_chip, (error_out, grad_out) = refs[:-2], refs[-2:]
-    width = from_chip[0].shape[2]
-    group = 2
-    for r in range(0, inc.shape[0], group):
-        rows = slice(r, r + group)
-        for part, ref in enumerate(from_chip):
-            lanes = slice(part * width, (part + 1) * width)
-            x = ref[rows].astype(jnp.float32)
-            d = from_core[rows, :, lanes].astype(jnp.float32)
-            error_out[rows, :, lanes] = inc[rows, :, lanes] - jnp.where(odd, d, x)
-            grad_out[rows, :, lanes] = base[rows, :, lanes] - jnp.where(odd, x, d)
-
-
-def final(increment, base, from_core, from_chip):
-    rows, across, levels = increment.shape
-    block = pl.BlockSpec((4, across, levels), lambda i: (i, 0, 0))
-    part = pl.BlockSpec((4, across, levels // len(from_chip)), lambda i: (i, 0, 0))
+    copies = []
+    for start in range(0, inc.shape[0], CHUNK):
+        for r in range(start, start + CHUNK):
+            x = from_chip[r].astype(jnp.float32)
+            d = from_core[r].astype(jnp.float32)
+            error[r] = inc[r] - jnp.where(odd, d, x)
+            grad[r] = base[r] - jnp.where(odd, x, d)
+        rows = pl.ds(start, CHUNK)
+        for f, (held, out) in enumerate(((error, error_out), (grad, grad_out))):
+            copies.append(pltpu.make_async_copy(held.at[rows], out.at[rows], sems.at[f, start // CHUNK]))
+            copies[-1].start()
+    for copy in copies:
+        copy.wait()
+
+
+def final(increment, base, from_chip, from_core):
+    hbm, vmem = pl.BlockSpec(memory_space=pltpu.HBM), pl.BlockSpec(memory_space=pltpu.VMEM)
     return pl.pallas_call(
         final_kernel,
-        grid=(rows // 4,),
-        in_specs=[block] * 3 + [part] * len(from_chip),
-        out_specs=[block] * 2,
+        in_specs=[vmem] * 4,
+        out_specs=[hbm] * 2,
         out_shape=[jax.ShapeDtypeStruct(increment.shape, jnp.float32)] * 2,
+        scratch_shapes=[pltpu.VMEM(increment.shape, jnp.float32)] * 2
+        + [pltpu.SemaphoreType.DMA((2, increment.shape[0] // CHUNK))],
         compiler_params=pltpu.CompilerParams(vmem_limit_bytes=16 << 20),
         cost_estimate=pl.CostEstimate(flops=4_000_000, bytes_accessed=10 << 20, transcendentals=0),
         name="final",
-    )(increment, base, from_core, *from_chip)
+    )(increment, base, from_chip, from_core)
 
 
 ROWS_BY_COLS = (((1,), (1,)), ((), ()))
@@ -411,15 +411,11 @@
     pieces = [above, below, across, above_corner, below_corner]
     tangent, token = spread(my_count, obs_column[0], tangents, token)
     tiles = levels // LANES
-    from_chip = []
-    for part in range(PARTS):
-        crossing, token = transported(
-            True, part * tiles // PARTS, tiles // PARTS, increment, multiplier, pieces, transport, token
-        )
-        from_chip.append(sent(crossing, lambda s, a, o: (s + 1 if s % 2 else s - 1, a, o)))
+    crossing, token = transported(True, 0, tiles, increment, multiplier, pieces, transport, token)
+    from_chip = sent(crossing, lambda s, a, o: (s + 1 if s % 2 else s - 1, a, o))
     staying, _ = transported(False, 0, tiles, increment, multiplier, pieces, transport, token)
     from_core = sent(staying, lambda s, a, o: (s - 1 if s % 2 else s + 1, a, o))
-    model_error, gradient = final(increment, base.reshape(increment.shape), from_core, from_chip)
+    model_error, gradient = final(increment, base.reshape(increment.shape), from_chip, from_core)
     return (model_error[None], gradient[None], tangent[None, None])
 
 

time: 92.4 us -> 82.2 us (0.89)
  the two profiles are of different devices: /device:TPU:13 before, /device:TPU:11 now
where the time goes in v3:
time: 82.2 us; the launch traced here: 81.9 us
  Pallas kernels  38.2 us (46%)
  starting transfers between devices  22.6 us (27%)
  waiting for transfers between devices  19.4 us (24%)
  between operations  0.97 us (1%)
    ppermute x7, starting transfers between devices, sent(): return lax.ppermute(array, ('sub', 'lat', 'lon'), pairs)  22.6 us
    ppermute x7, waiting for transfers between devices, sent(): return lax.ppermute(array, ('sub', 'lat', 'lon'), pairs)  19.4 us
    pallas_call x2, Pallas kernels, transported(): pl.pallas_call(functools.partial(transport_kernel, crossing, low_tile), i...  16.7 us
    pallas_call x1, Pallas kernels, network(): pl.pallas_call(network_kernel, in_specs=[pl.BlockSpec(memory_space=pltpu....  12.1 us
    pallas_call x1, Pallas kernels, spread(): pl.pallas_call(spread_kernel, in_specs=[pl.BlockSpec(memory_space=pltpu.S...  3.92 us
    pallas_call x1, Pallas kernels, pack(): pl.pallas_call(pack_kernel, in_specs=[pl.BlockSpec(memory_space=pltpu.HBM...  3.31 us
    pallas_call x1, Pallas kernels, final(): pl.pallas_call(final_kernel, in_specs=[vmem] * 4, out_specs=[hbm] * 2, ou...  2.18 us
  transfers between devices with their start and end apart: 7, of which 2 were waited for; matrix products, arithmetic and copies ran while one was open for 1% of the time, Pallas kernels for 30%

profile of v3, /device:TPU:11, one launch (start us, length us, event | category | flops | bytes accessed | tf_op | source)
XLA Modules:
  0.0 81.9 jit_solution(12313522514331037240)
XLA Ops:
  0.6 0.0 copy-start
  0.6 0.0 copy-start.3
  0.7 0.0 copy-start.4
  0.7 3.3 %pack.1 = (bf16[2,8,64,512]{3,2,1,0:T(8,128)(2,1)S(1)}, bf16[2,8,64,512]{3,2,1,0:T(8,128)(2,1)}, bf16[2,16,8,512]{3,2,1,0:T(8,128)(2,1)}) custom-call(f32[16,64,512]{2,1,0:T(8,128)} %bitcast.13, f32[16,64,512]{2,1,0:T(8,128)} %bitcast.22), custom_call_target="tpu_custom_call" | custom-call | tf_op jit(solution)/shard_map/pack/pallas_call | solution.py:53
  4.0 3.5 %collective-permute-start = (bf16[2,8,64,512]{3,2,1,0:T(8,128)(2,1)}, bf16[2,8,64,512]{3,2,1,0:T(8,128)(2,1)S(1)}, u32[]{:S(2)}, u32[]{:S(2)}) collective-permute-start(bf16[2,8,64,512]{3,2,1,0:T(8,128)(2,1)} %get-tuple-element.20), channel_id=1, source_target_pairs={{0,2},{1,3},{2,4},{3,5},{4,6},{5,7},{6,8},{7,9},{8,10},{9,11},{10,... | collective-permute-start | bytes 3145736 | tf_op jit(solution)/shard_map/ppermute | solution.py:374
  7.5 3.9 %collective-permute-start.1 = (bf16[2,8,64,512]{3,2,1,0:T(8,128)(2,1)S(1)}, bf16[2,8,64,512]{3,2,1,0:T(8,128)(2,1)S(1)}, u32[]{:S(2)}, u32[]{:S(2)}) collective-permute-start(bf16[2,8,64,512]{3,2,1,0:T(8,128)(2,1)S(1)} %get-tuple-element.21), channel_id=1, source_target_pairs={{2,0},{3,1},{4,2},{5,3},{6,4},{7,5},{8,6},{9,7},{10,8},{11,9},{12,... | collective-permute-start | bytes 3145736 | tf_op jit(solution)/shard_map/ppermute | solution.py:374
  11.5 2.4 %collective-permute-start.2 = (bf16[2,16,8,512]{3,2,1,0:T(8,128)(2,1)}, bf16[2,16,8,512]{3,2,1,0:T(8,128)(2,1)S(1)}, u32[]{:S(2)}, u32[]{:S(2)}) collective-permute-start(bf16[2,16,8,512]{3,2,1,0:T(8,128)(2,1)} %get-tuple-element.22), channel_id=1, source_target_pairs={{0,1},{1,0},{2,3},{3,2},{4,5},{5,4},{6,7},{7,6},{8,9},{9,8},{10,11... | collective-permute-start | bytes 786440 | tf_op jit(solution)/shard_map/ppermute | solution.py:374
  13.9 0.0 copy-done
  13.9 0.7 constant_dynamic-slice_fusion
  14.5 0.0 copy-done.3
  14.5 0.0 copy-done.4
  14.5 12.1 %network.1 = (bf16[1024,512]{1,0:T(8,128)(2,1)S(1)}, f32[1024,512]{1,0:T(8,128)S(1)}, f32[8,128]{1,0:T(8,128)S(1)}) custom-call(s32[1]{0:T(128)} %bitcast.1.count, s32[1,2048]{1,0:T(1,128)S(1)} %bitcast.19, f32[1,1024]{1,0:T(1,128)S(1)} %bitcast.21, f32[1024,512]{1,0:T(8,128)} %bitcast.14, bf16[1024,512]{1,0:T(8,128)(2,1)} %bitcast.29, ...), custom_call_target="tpu_custom_call" | custom-call | flops 7516192768 | bytes 12582912 | tf_op jit(solution)/shard_map/network/pallas_call | solution.py:303
  26.6 15.3 %collective-permute-done.2.strip = bf16[2,16,8,512]{3,2,1,0:T(8,128)(2,1)S(1)} collective-permute-done((bf16[2,16,8,512]{3,2,1,0:T(8,128)(2,1)}, bf16[2,16,8,512]{3,2,1,0:T(8,128)(2,1)S(1)}, u32[]{:S(2)}, u32[]{:S(2)}) %collective-permute-start.2) | collective-permute-done | bytes 262176 | tf_op jit(solution)/shard_map/ppermute | solution.py:374
  42.0 1.9 %collective-permute-start.3 = (bf16[2,6,8,512]{3,2,1,0:T(8,128)(2,1)S(1)}, bf16[2,6,8,512]{3,2,1,0:T(8,128)(2,1)S(1)}, u32[]{:S(2)}, u32[]{:S(2)}) collective-permute-start(bf16[2,6,8,512]{3,2,1,0:T(8,128)(2,1)S(1)} %get-tuple-element.24), channel_id=1, source_target_pairs={{0,2},{1,3},{2,4},{3,5},{4,6},{5,7},{6,8},{7,9},{8,10},{9,11},{10,... | collective-permute-start | bytes 294920 | tf_op jit(solution)/shard_map/ppermute | solution.py:374
  43.9 5.7 %collective-permute-start.4 = (bf16[2,6,8,512]{3,2,1,0:T(8,128)(2,1)S(1)}, bf16[2,6,8,512]{3,2,1,0:T(8,128)(2,1)S(1)}, u32[]{:S(2)}, u32[]{:S(2)}) collective-permute-start(bf16[2,6,8,512]{3,2,1,0:T(8,128)(2,1)S(1)} %get-tuple-element.25), channel_id=1, source_target_pairs={{2,0},{3,1},{4,2},{5,3},{6,4},{7,5},{8,6},{9,7},{10,8},{11,9},{12,... | collective-permute-start | bytes 294920 | tf_op jit(solution)/shard_map/ppermute | solution.py:374
  49.6 0.0 copy-start.2
  49.6 3.9 %spread.1 = (bf16[2048,512]{1,0:T(8,128)(2,1)}, f32[8,128]{1,0:T(8,128)S(1)}) custom-call(s32[1]{0:T(128)} %bitcast.1.count, s32[1,2048]{1,0:T(1,128)S(1)} %bitcast.20, bf16[1024,512]{1,0:T(8,128)(2,1)S(1)} %get-tuple-element.26.tangents, f32[8,128]{1,0:T(8,128)S(1)} %get-tuple-element.27._), custom_call_target="tpu_custom_call" | custom-call | flops 2147483648 | bytes 4194304 | tf_op jit(solution)/shard_map/spread/pallas_call | solution.py:349
  53.5 0.0 collective-permute-done.3.above_corner
  53.5 0.0 collective-permute-done.4.below_corner
  53.5 0.0 collective-permute-done.above
  53.5 0.0 collective-permute-done.1.below
  53.5 0.0 copy-done.2
  53.5 8.2 %crossing.1 = (bf16[16,64,512]{2,1,0:T(8,128)(2,1)S(1)}, f32[8,128]{1,0:T(8,128)S(1)}) custom-call(f32[16,64,512]{2,1,0:T(8,128)} %bitcast.15, f32[16,64,512]{2,1,0:T(8,128)} %bitcast.24, bf16[2,8,64,512]{3,2,1,0:T(8,128)(2,1)S(1)} %collective-permute-done.above, bf16[2,8,64,512]{3,2,1,0:T(8,128)(2,1)S(1)} %collective-permute-done.1.below, ...), custom_call_target="tpu_custom_call" | custom-call | flops 50000000 | bytes 4194304 | tf_op jit(solution)/shard_map/crossing/pallas_call | solution.py:197
  61.7 5.1 %collective-permute-start.5 = (bf16[16,64,512]{2,1,0:T(8,128)(2,1)S(1)}, bf16[16,64,512]{2,1,0:T(8,128)(2,1)S(1)}, u32[]{:S(2)}, u32[]{:S(2)}) collective-permute-start(bf16[16,64,512]{2,1,0:T(8,128)(2,1)S(1)} %get-tuple-element.29), channel_id=1, source_target_pairs={{16,32},{17,33},{18,34},{19,35},{20,36},{21,37},{22,38},{23,39},{2... | collective-permute-start | bytes 3145736 | tf_op jit(solution)/shard_map/ppermute | solution.py:374
  66.8 0.0 copy-start.1
  66.8 8.6 %staying.1 = (bf16[16,64,512]{2,1,0:T(8,128)(2,1)S(1)}, f32[8,128]{1,0:T(8,128)}) custom-call(f32[16,64,512]{2,1,0:T(8,128)} %bitcast.16, f32[16,64,512]{2,1,0:T(8,128)} %bitcast.25, bf16[2,8,64,512]{3,2,1,0:T(8,128)(2,1)S(1)} %collective-permute-done.above, bf16[2,8,64,512]{3,2,1,0:T(8,128)(2,1)S(1)} %collective-permute-done.1.below, ...), custom_call_target="tpu_custom_call" | custom-call | flops 50000000 | bytes 4194304 | tf_op jit(solution)/shard_map/staying/pallas_call | solution.py:197
  75.4 0.1 collective-permute-start.6
  75.5 4.0 %collective-permute-done.5.from_chip = bf16[16,64,512]{2,1,0:T(8,128)(2,1)S(1)} collective-permute-done((bf16[16,64,512]{2,1,0:T(8,128)(2,1)S(1)}, bf16[16,64,512]{2,1,0:T(8,128)(2,1)S(1)}, u32[]{:S(2)}, u32[]{:S(2)}) %collective-permute-start.5) | collective-permute-done | bytes 1048608 | tf_op jit(solution)/shard_map/ppermute | solution.py:374
  79.5 0.0 collective-permute-done.6.from_core
  79.6 0.0 copy-done.1
  79.6 2.2 %final.1 = (f32[16,64,512]{2,1,0:T(8,128)}, f32[16,64,512]{2,1,0:T(8,128)}) custom-call(f32[16,64,512]{2,1,0:T(8,128)S(1)} %bitcast.17, f32[16,64,512]{2,1,0:T(8,128)S(1)} %bitcast.18, bf16[16,64,512]{2,1,0:T(8,128)(2,1)S(1)} %collective-permute-done.5.from_chip, bf16[16,64,512]{2,1,0:T(8,128)(2,1)S(1)} %collective-permute-done.6.from_core), custom_call_target="tpu_custom_call" | custom-call | flops 4000000 | bytes 10485760 | tf_op jit(solution)/shard_map/final/pallas_call | solution.py:232
  (1 shorter events, 0.0 us)
Async XLA Ops:
  0.6 13.2 %copy-start = (s32[1,16]{1,0:T(1,128)S(1)}, s32[1,16]{1,0:T(1,128)}, u32[]{:S(2)}) copy-start(s32[1,16]{1,0:T(1,128)} %param.15) | copy-start | bytes 196
  0.6 13.9 %copy-start.3 = (s32[1,1,2048]{2,1,0:T(1,128)S(1)}, s32[1,1,2048]{2,1,0:T(1,128)}, u32[]{:S(2)}) copy-start(s32[1,1,2048]{2,1,0:T(1,128)} %param.14) | copy-start | bytes 24580
  0.7 13.9 %copy-start.4 = (f32[1024]{0:T(1024)S(1)}, f32[1024]{0:T(1024)}, u32[]{:S(2)}) copy-start(f32[1024]{0:T(1024)} %param.18) | copy-start | bytes 12292
  4.0 49.5 %collective-permute-start = (bf16[2,8,64,512]{3,2,1,0:T(8,128)(2,1)}, bf16[2,8,64,512]{3,2,1,0:T(8,128)(2,1)S(1)}, u32[]{:S(2)}, u32[]{:S(2)}) collective-permute-start(bf16[2,8,64,512]{3,2,1,0:T(8,128)(2,1)} %get-tuple-element.20), channel_id=1, source_target_pairs={{0,2},{1,3},{2,4},{3,5},{4,6},{5,7},{6,8},{7,9},{8,10},{9,11},{10,... | collective-permute-start | bytes 3145736 | tf_op jit(solution)/shard_map/ppermute | solution.py:374
  7.5 46.0 %collective-permute-start.1 = (bf16[2,8,64,512]{3,2,1,0:T(8,128)(2,1)S(1)}, bf16[2,8,64,512]{3,2,1,0:T(8,128)(2,1)S(1)}, u32[]{:S(2)}, u32[]{:S(2)}) collective-permute-start(bf16[2,8,64,512]{3,2,1,0:T(8,128)(2,1)S(1)} %get-tuple-element.21), channel_id=1, source_target_pairs={{2,0},{3,1},{4,2},{5,3},{6,4},{7,5},{8,6},{9,7},{10,8},{11,9},{12,... | collective-permute-start | bytes 3145736 | tf_op jit(solution)/shard_map/ppermute | solution.py:374
  11.5 30.5 %collective-permute-start.2 = (bf16[2,16,8,512]{3,2,1,0:T(8,128)(2,1)}, bf16[2,16,8,512]{3,2,1,0:T(8,128)(2,1)S(1)}, u32[]{:S(2)}, u32[]{:S(2)}) collective-permute-start(bf16[2,16,8,512]{3,2,1,0:T(8,128)(2,1)} %get-tuple-element.22), channel_id=1, source_target_pairs={{0,1},{1,0},{2,3},{3,2},{4,5},{5,4},{6,7},{7,6},{8,9},{9,8},{10,11... | collective-permute-start | bytes 786440 | tf_op jit(solution)/shard_map/ppermute | solution.py:374
  42.0 11.5 %collective-permute-start.3 = (bf16[2,6,8,512]{3,2,1,0:T(8,128)(2,1)S(1)}, bf16[2,6,8,512]{3,2,1,0:T(8,128)(2,1)S(1)}, u32[]{:S(2)}, u32[]{:S(2)}) collective-permute-start(bf16[2,6,8,512]{3,2,1,0:T(8,128)(2,1)S(1)} %get-tuple-element.24), channel_id=1, source_target_pairs={{0,2},{1,3},{2,4},{3,5},{4,6},{5,7},{6,8},{7,9},{8,10},{9,11},{10,... | collective-permute-start | bytes 294920 | tf_op jit(solution)/shard_map/ppermute | solution.py:374
  43.9 9.6 %collective-permute-start.4 = (bf16[2,6,8,512]{3,2,1,0:T(8,128)(2,1)S(1)}, bf16[2,6,8,512]{3,2,1,0:T(8,128)(2,1)S(1)}, u32[]{:S(2)}, u32[]{:S(2)}) collective-permute-start(bf16[2,6,8,512]{3,2,1,0:T(8,128)(2,1)S(1)} %get-tuple-element.25), channel_id=1, source_target_pairs={{2,0},{3,1},{4,2},{5,3},{6,4},{7,5},{8,6},{9,7},{10,8},{11,9},{12,... | collective-permute-start | bytes 294920 | tf_op jit(solution)/shard_map/ppermute | solution.py:374
  49.6 4.0 %copy-start.2 = (f32[8,512]{1,0:T(8,128)S(1)}, f32[8,512]{1,0:T(8,128)}, u32[]{:S(2)}) copy-start(f32[8,512]{1,0:T(8,128)} %rates.3) | copy-start | bytes 49156
  61.7 17.8 %collective-permute-start.5 = (bf16[16,64,512]{2,1,0:T(8,128)(2,1)S(1)}, bf16[16,64,512]{2,1,0:T(8,128)(2,1)S(1)}, u32[]{:S(2)}, u32[]{:S(2)}) collective-permute-start(bf16[16,64,512]{2,1,0:T(8,128)(2,1)S(1)} %get-tuple-element.29), channel_id=1, source_target_pairs={{16,32},{17,33},{18,34},{19,35},{20,36},{21,37},{22,38},{23,39},{2... | collective-permute-start | bytes 3145736 | tf_op jit(solution)/shard_map/ppermute | solution.py:374
  66.8 12.7 %copy-start.1 = (f32[1,16,64,512]{3,2,1,0:T(8,128)S(1)}, f32[1,16,64,512]{3,2,1,0:T(8,128)}, u32[]{:S(2)}) copy-start(f32[1,16,64,512]{3,2,1,0:T(8,128)} %param.10) | copy-start | bytes 6291460
  75.4 4.1 %collective-permute-start.6 = (bf16[16,64,512]{2,1,0:T(8,128)(2,1)S(1)}, bf16[16,64,512]{2,1,0:T(8,128)(2,1)S(1)}, u32[]{:S(2)}, u32[]{:S(2)}) collective-permute-start(bf16[16,64,512]{2,1,0:T(8,128)(2,1)S(1)} %get-tuple-element.31), channel_id=1, source_target_pairs={{0,16},{1,17},{2,18},{3,19},{4,20},{5,21},{6,22},{7,23},{8,24},{9,... | collective-permute-start | bytes 3145736 | tf_op jit(solution)/shard_map/ppermute | solution.py:374

commit v4 on v3

--- a/solution.py
+++ b/solution.py
@@ -1,5 +1,3 @@
-import functools
-
 import jax
 import jax.numpy as jnp
 from jax import lax
@@ -101,113 +99,228 @@
                 dst[i + r, j : j + 8, :] = total
 
 
-def transport_kernel(
-    crossing, low_tile, inc, mul, above, below, strip, above_corner, below_corner, rates, _, out, token, bufs, other, sems
-):
-    lat, lon = lax.axis_index("lat"), lax.axis_index("lon")
-    odd = lax.rem(lax.axis_index("sub"), 2)
-    n_lat = lax.axis_size("lat")
-    rows, across = inc.shape[0], inc.shape[1]
-    tall = rows + 2 * REACH
-    blocks = (across + REACH) // 8
-    tiles = bufs.shape[0]
+def geometry(across):
+    lon = lax.axis_index("lon")
     own = pl.multiple_of(8 + REACH * lon, 8)
     beside = pl.multiple_of(8 + across * (1 - lon), 8)
-    f = 1 - odd if crossing else odd
-    forward = f == 0
-
-    def arriving(src, t):
-        there = bufs.at[t, pl.ds(REACH, rows), pl.ds(own, across), :]
-        return pltpu.make_async_copy(src.at[:, :, pl.ds((low_tile + t) * LANES, LANES)], there, sems.at[t])
+    return own, beside, (across + REACH) // 8
+
+
+def is_forward(crossing):
+    odd = lax.rem(lax.axis_index("sub"), 2)
+    return (1 - odd if crossing else odd) == 0
+
+
+def place_block(forward, inc, mul, strip, bufs, sems):
+    rows, across = inc.shape[0], inc.shape[1]
+    own, beside, blocks = geometry(across)
+
+    def start(src):
+        for t in range(bufs.shape[0]):
+            there = bufs.at[t, pl.ds(REACH, rows), pl.ds(own, across), :]
+            pltpu.make_async_copy(src.at[:, :, pl.ds(t * LANES, LANES)], there, sems.at[t]).start()
 
     @pl.when(forward)
     def _():
-        for t in range(tiles):
-            arriving(inc, t).start()
+        start(inc)
 
     @pl.when(jnp.logical_not(forward))
     def _():
-        for t in range(tiles):
-            arriving(mul, t).start()
-
-    token[...] = jnp.zeros_like(token)
-    blank = jnp.zeros((8, LANES), jnp.float32)
-    for r in range(tall):
-        other[r] = jnp.zeros(other.shape[1:], jnp.float32)
-        for t in range(tiles):
-            bufs[t, r, 0:8, :] = blank
-            bufs[t, r, 8 * blocks + 8 : 8 * blocks + 16, :] = blank
-    for t in range(tiles):
+        start(mul)
+
+    f = jnp.where(forward, 0, 1)
+    for t in range(bufs.shape[0]):
+        for r in range(rows + 2 * REACH):
+            bufs[t, r, 0:8, :] = jnp.zeros((8, LANES), jnp.float32)
+            bufs[t, r, 8 * blocks + 8 : 8 * blocks + 16, :] = jnp.zeros((8, LANES), jnp.float32)
+        for r in range(rows):
+            lanes = slice(t * LANES, (t + 1) * LANES)
+            bufs[t, REACH + r, pl.ds(beside, REACH), :] = strip[f, r, :, lanes].astype(jnp.float32)
+
+
+def wait_block(inc, bufs, sems, t):
+    rows, across = inc.shape[0], inc.shape[1]
+    own, _, _ = geometry(across)
+    there = bufs.at[t, pl.ds(REACH, rows), pl.ds(own, across), :]
+    pltpu.make_async_copy(inc.at[:, :, pl.ds(0, LANES)], there, sems.at[t]).wait()
+
+
+def place_halo(forward, above, below, above_corner, below_corner, bufs):
+    tall, across = bufs.shape[1], above.shape[2]
+    rows = tall - 2 * REACH
+    own, beside, _ = geometry(across)
+    f = jnp.where(forward, 0, 1)
+    for t in range(bufs.shape[0]):
+        lanes = slice(t * LANES, (t + 1) * LANES)
         for r in (0, 1, tall - 2, tall - 1):
-            bufs[t, r, pl.ds(beside, REACH), :] = blank
+            bufs[t, r, pl.ds(beside, REACH), :] = jnp.zeros((REACH, LANES), jnp.float32)
         for r in range(REACH):
-            lanes = slice((low_tile + t) * LANES, (low_tile + t + 1) * LANES)
             bufs[t, r, pl.ds(own, across), :] = above[f, r, :, lanes].astype(jnp.float32)
             bufs[t, rows + REACH + r, pl.ds(own, across), :] = below[f, r, :, lanes].astype(jnp.float32)
-        for r in range(rows):
-            bufs[t, REACH + r, pl.ds(beside, REACH), :] = strip[f, r, :, lanes].astype(jnp.float32)
         for r in range(EDGE):
             bufs[t, REACH - EDGE + r, pl.ds(beside, REACH), :] = above_corner[f, r, :, lanes].astype(jnp.float32)
             bufs[t, rows + REACH + r, pl.ds(beside, REACH), :] = below_corner[f, r, :, lanes].astype(jnp.float32)
 
+
+def taps_of(forward, rates, t):
+    lanes = pl.ds(pl.multiple_of(t * LANES, LANES), LANES)
+    spread = [
+        jnp.broadcast_to(jnp.where(forward, rates[k : k + 1, lanes], rates[m : m + 1, lanes]), (8, LANES))
+        for k, m in enumerate(MIRROR)
+    ]
+    rest = spread[0]
+    for k in range(1, 8):
+        rest = rest + spread[k]
+    center = 1.0 - rest
+    return [c / center for c in spread], (center * center) * (center * center)
+
+
+def steps(a, b, taps, blocks, rows, ranges):
+    lat, n_lat = lax.axis_index("lat"), lax.axis_size("lat")
+    for spans in ranges:
+        for first, last in spans:
+            sweep(a, b, taps, first, last, blocks)
+        low, high = spans[0][0], spans[-1][1]
+        if low < REACH:
+
+            @pl.when(lat == 0)
+            def _(b=b, low=low):
+                for r in range(low, REACH):
+                    b[r] = jnp.zeros(b.shape[1:], jnp.float32)
+
+            @pl.when(lat == n_lat - 1)
+            def _(b=b, high=high):
+                for r in range(rows + REACH, high):
+                    b[r] = jnp.zeros(b.shape[1:], jnp.float32)
+
+        a, b = b, a
+    return a
+
+
+def write_tile(out, done, scale, t, rows, across):
+    own, _, _ = geometry(across)
+    lanes = pl.ds(pl.multiple_of(t * LANES, LANES), LANES)
+    for r in range(rows):
+        out[r, :, lanes] = (scale[0:1] * done[REACH + r, pl.ds(own, across), :]).astype(jnp.bfloat16)
+
+
+def whole_kernel(inc, mul, above, below, strip, above_corner, below_corner, rates, _, out, token, bufs, other, sems):
+    rows, across = inc.shape[0], inc.shape[1]
+    blocks = (across + REACH) // 8
+    tall = rows + 2 * REACH
+    forward = is_forward(False)
+    place_block(forward, inc, mul, strip, bufs, sems)
+    token[...] = jnp.zeros_like(token)
+    place_halo(forward, above, below, above_corner, below_corner, bufs)
+    for r in range(tall):
+        other[r] = jnp.zeros(other.shape[1:], jnp.float32)
+    ranges = [[(2 * k, tall - 2 * k)] for k in range(1, STEPS + 1)]
+
     def tile_of(t, carry):
-        lanes = pl.ds(pl.multiple_of((low_tile + t) * LANES, LANES), LANES)
-        out_lanes = pl.ds(pl.multiple_of(t * LANES, LANES), LANES)
-        pltpu.make_async_copy(
-            inc.at[:, :, lanes], bufs.at[t, pl.ds(REACH, rows), pl.ds(own, across), :], sems.at[t]
-        ).wait()
-        spread = [
-            jnp.broadcast_to(jnp.where(forward, rates[k : k + 1, lanes], rates[m : m + 1, lanes]), (8, LANES))
-            for k, m in enumerate(MIRROR)
-        ]
-        rest = spread[0]
-        for k in range(1, 8):
-            rest = rest + spread[k]
-        center = 1.0 - rest
-        taps = [c / center for c in spread]
-        scale = (center * center) * (center * center)
-        a, b = bufs.at[t], other
-        for step in range(STEPS):
-            first, last = 2 * (step + 1), tall - 2 * (step + 1)
-            sweep(a, b, taps, first, last, blocks)
-            if step < STEPS - 1:
-
-                @pl.when(lat == 0)
-                def _(b=b, first=first):
-                    for r in range(first, REACH):
-                        b[r] = jnp.zeros(b.shape[1:], jnp.float32)
-
-                @pl.when(lat == n_lat - 1)
-                def _(b=b, last=last):
-                    for r in range(rows + REACH, last):
-                        b[r] = jnp.zeros(b.shape[1:], jnp.float32)
-
-            a, b = b, a
-        for r in range(rows):
-            out[r, :, out_lanes] = (scale[0:1] * a[REACH + r, pl.ds(own, across), :]).astype(jnp.bfloat16)
+        wait_block(inc, bufs, sems, t)
+        taps, scale = taps_of(forward, rates, t)
+        done = steps(bufs.at[t], other, taps, blocks, rows, ranges)
+        write_tile(out, done, scale, t, rows, across)
         return carry
 
-    lax.fori_loop(0, tiles, tile_of, 0)
-
-
-def transported(crossing, low_tile, tiles, increment, multiplier, pieces, rates, token):
-    rows, across, _ = increment.shape
-    tall, wide = rows + 2 * REACH, across + REACH + 16
-    hbm, vmem = pl.BlockSpec(memory_space=pltpu.HBM), pl.BlockSpec(memory_space=pltpu.VMEM)
-    return pl.pallas_call(
-        functools.partial(transport_kernel, crossing, low_tile),
-        in_specs=[hbm, hbm] + [vmem] * (len(pieces) + 1) + [pl.BlockSpec(memory_space=pl.ANY)],
-        out_specs=[vmem, vmem],
-        out_shape=[jax.ShapeDtypeStruct((rows, across, tiles * LANES), jnp.bfloat16), TOKEN],
+    lax.fori_loop(0, bufs.shape[0], tile_of, 0)
+
+
+def inner_kernel(inc, mul, strip, rates, _, bufs, other, sems):
+    rows, across = inc.shape[0], inc.shape[1]
+    blocks = (across + REACH) // 8
+    forward = is_forward(True)
+    place_block(forward, inc, mul, strip, bufs, sems)
+    for t in range(bufs.shape[0]):
+        for r in range(rows + 2 * REACH):
+            other[t, r, 0:8, :] = jnp.zeros((8, LANES), jnp.float32)
+            other[t, r, 8 * blocks + 8 : 8 * blocks + 16, :] = jnp.zeros((8, LANES), jnp.float32)
+    ranges = [[(REACH + 2 * k, REACH + rows - 2 * k)] for k in range(1, STEPS)]
+
+    def tile_of(t, carry):
+        wait_block(inc, bufs, sems, t)
+        taps, _ = taps_of(forward, rates, t)
+        steps(bufs.at[t], other.at[t], taps, blocks, rows, ranges)
+        return carry
+
+    lax.fori_loop(0, bufs.shape[0], tile_of, 0)
+
+
+def outer_kernel(above, below, above_corner, below_corner, rates, _, __, out, bufs, other):
+    rows, across = out.shape[0], out.shape[1]
+    blocks = (across + REACH) // 8
+    tall = rows + 2 * REACH
+    forward = is_forward(True)
+    place_halo(forward, above, below, above_corner, below_corner, bufs)
+    ranges = [
+        [(2 * k, REACH + 2 * k), (REACH + rows - 2 * k, tall - 2 * k)] if k < STEPS else [(2 * k, tall - 2 * k)]
+        for k in range(1, STEPS + 1)
+    ]
+
+    def tile_of(t, carry):
+        taps, scale = taps_of(forward, rates, t)
+        done = steps(bufs.at[t], other.at[t], taps, blocks, rows, ranges)
+        write_tile(out, done, scale, t, rows, across)
+        return carry
+
+    lax.fori_loop(0, bufs.shape[0], tile_of, 0)
+
+
+HBM = pl.BlockSpec(memory_space=pltpu.HBM)
+VMEM = pl.BlockSpec(memory_space=pltpu.VMEM)
+ANY = pl.BlockSpec(memory_space=pl.ANY)
+
+
+def staying_field(increment, multiplier, pieces, rates, token):
+    rows, across, levels = increment.shape
+    tall, wide, tiles = rows + 2 * REACH, across + REACH + 16, levels // LANES
+    return pl.pallas_call(
+        whole_kernel,
+        in_specs=[HBM, HBM] + [VMEM] * (len(pieces) + 1) + [ANY],
+        out_specs=[VMEM, VMEM],
+        out_shape=[jax.ShapeDtypeStruct(increment.shape, jnp.bfloat16), TOKEN],
         scratch_shapes=[
             pltpu.VMEM((tiles, tall, wide, LANES), jnp.float32),
             pltpu.VMEM((tall, wide, LANES), jnp.float32),
             pltpu.SemaphoreType.DMA((tiles,)),
         ],
         compiler_params=pltpu.CompilerParams(vmem_limit_bytes=24 << 20),
-        cost_estimate=pl.CostEstimate(flops=12_500_000 * tiles, bytes_accessed=tiles << 20, transcendentals=0),
-        name="crossing" if crossing else "staying",
+        cost_estimate=pl.CostEstimate(flops=50_000_000, bytes_accessed=4 << 20, transcendentals=0),
+        name="staying",
     )(*in_hbm(increment, multiplier), *pieces, rates, token)
+
+
+def crossing_inner(increment, multiplier, strip, rates, token):
+    rows, across, levels = increment.shape
+    tall, wide, tiles = rows + 2 * REACH, across + REACH + 16, levels // LANES
+    return pl.pallas_call(
+        inner_kernel,
+        in_specs=[HBM, HBM, VMEM, VMEM, ANY],
+        out_specs=[VMEM] * 2,
+        out_shape=[jax.ShapeDtypeStruct((tiles, tall, wide, LANES), jnp.float32)] * 2,
+        scratch_shapes=[pltpu.SemaphoreType.DMA((tiles,))],
+        compiler_params=pltpu.CompilerParams(vmem_limit_bytes=20 << 20),
+        cost_estimate=pl.CostEstimate(flops=14_000_000, bytes_accessed=2 << 20, transcendentals=0),
+        name="inner",
+    )(*in_hbm(increment, multiplier), strip, rates, token)
+
+
+def crossing_outer(pieces, rates, bufs, other, shape):
+    above, below, _, above_corner, below_corner = pieces
+    return pl.pallas_call(
+        outer_kernel,
+        in_specs=[VMEM] * 7,
+        out_specs=[VMEM] * 3,
+        out_shape=[
+            jax.ShapeDtypeStruct(shape, jnp.bfloat16),
+            jax.ShapeDtypeStruct(bufs.shape, jnp.float32),
+            jax.ShapeDtypeStruct(other.shape, jnp.float32),
+        ],
+        input_output_aliases={5: 1, 6: 2},
+        compiler_params=pltpu.CompilerParams(vmem_limit_bytes=20 << 20),
+        cost_estimate=pl.CostEstimate(flops=36_000_000, bytes_accessed=2 << 20, transcendentals=0),
+        name="outer",
+    )(above, below, above_corner, below_corner, rates, bufs, other)[0]
 
 
 def final_kernel(inc, base, from_chip, from_core, error_out, grad_out, error, grad, sems):
@@ -321,9 +434,8 @@
     )(count, columns, hidden_bias, *in_hbm(*moved))
 
 
-def spread_kernel(count, columns, tangents, _, out, token, held, sems):
+def spread_kernel(count, columns, tangents, _, out, held, sems):
     slots, cols = held.shape[0], tangents.shape[0]
-    token[...] = jnp.zeros_like(token)
     lane = lax.broadcasted_iota(jnp.int32, (LANES, LANES), 1)
     outs = []
     for i, start in enumerate(range(0, slots, SLOTS_TILE)):
@@ -349,8 +461,8 @@
     return pl.pallas_call(
         spread_kernel,
         in_specs=[pl.BlockSpec(memory_space=pltpu.SMEM), vmem, vmem, pl.BlockSpec(memory_space=pl.ANY)],
-        out_specs=[pl.BlockSpec(memory_space=pltpu.HBM), vmem],
-        out_shape=[jax.ShapeDtypeStruct((slots, chan), jnp.bfloat16), TOKEN],
+        out_specs=pl.BlockSpec(memory_space=pltpu.HBM),
+        out_shape=jax.ShapeDtypeStruct((slots, chan), jnp.bfloat16),
         scratch_shapes=[
             pltpu.VMEM((slots, chan), jnp.bfloat16),
             pltpu.SemaphoreType.DMA((slots // SLOTS_TILE,)),
@@ -409,12 +521,13 @@
     above_corner = sent(high_corner, lambda s, a, o: (s, a + 1, o))
     below_corner = sent(low_corner, lambda s, a, o: (s, a - 1, o))
     pieces = [above, below, across, above_corner, below_corner]
-    tangent, token = spread(my_count, obs_column[0], tangents, token)
-    tiles = levels // LANES
-    crossing, token = transported(True, 0, tiles, increment, multiplier, pieces, transport, token)
+    pieces = [above, below, across, above_corner, below_corner]
+    bufs, other = crossing_inner(increment, multiplier, across, transport, token)
+    crossing = crossing_outer(pieces, transport, bufs, other, increment.shape)
     from_chip = sent(crossing, lambda s, a, o: (s + 1 if s % 2 else s - 1, a, o))
-    staying, _ = transported(False, 0, tiles, increment, multiplier, pieces, transport, token)
+    staying, token = staying_field(increment, multiplier, pieces, transport, token)
     from_core = sent(staying, lambda s, a, o: (s - 1 if s % 2 else s + 1, a, o))
+    tangent = spread(my_count, obs_column[0], tangents, token)
     model_error, gradient = final(increment, base.reshape(increment.shape), from_chip, from_core)
     return (model_error[None], gradient[None], tangent[None, None])
 

time: 82.2 us -> 78.4 us (0.954)
  waiting for transfers between devices: 19.4 us -> 15.6 us
    ppermute x7, waiting for transfers between devices: 19.4 us -> 15.6 us  [sent(): return lax.ppermute(array, ('sub', 'lat', 'lon'), pairs)]
    pallas_call x2 -> x3, Pallas kernels: 16.7 us -> 16.6 us  [the longest x1 8.18 us: staying_field(): pl.pallas_call(whole_kernel, in_specs=[HBM, HBM] + [VMEM] * (len(pieces)...]
  transfers between devices with their start and end apart: 7 -> 7, of which waited for: 2 -> 2; matrix products, arithmetic and copies ran while one was open for 1% -> 1% of each run, Pallas kernels for 30% -> 35%
where the time goes in v4:
time: 78.4 us; the launch traced here: 78 us
  Pallas kernels  38.2 us (49%)
  starting transfers between devices  22.6 us (29%)
  waiting for transfers between devices  15.6 us (20%)
  between operations  0.96 us (1%)
    ppermute x7, starting transfers between devices, sent(): return lax.ppermute(array, ('sub', 'lat', 'lon'), pairs)  22.6 us
    ppermute x7, waiting for transfers between devices, sent(): return lax.ppermute(array, ('sub', 'lat', 'lon'), pairs)  15.6 us
    pallas_call x1, Pallas kernels, network(): pl.pallas_call(network_kernel, in_specs=[pl.BlockSpec(memory_space=pltpu....  12.1 us
    pallas_call x1, Pallas kernels, staying_field(): pl.pallas_call(whole_kernel, in_specs=[HBM, HBM] + [VMEM] * (len(pieces)...  8.18 us
    pallas_call x1, Pallas kernels, crossing_outer(): pl.pallas_call(outer_kernel, in_specs=[VMEM] * 7, out_specs=[VMEM] * 3, o...  5.38 us
    pallas_call x1, Pallas kernels, spread(): pl.pallas_call(spread_kernel, in_specs=[pl.BlockSpec(memory_space=pltpu.S...  4.01 us
    pallas_call x1, Pallas kernels, pack(): pl.pallas_call(pack_kernel, in_specs=[pl.BlockSpec(memory_space=pltpu.HBM...  3.31 us
    pallas_call x1, Pallas kernels, crossing_inner(): pl.pallas_call(inner_kernel, in_specs=[HBM, HBM, VMEM, VMEM, ANY], out_sp...  3.03 us
  transfers between devices with their start and end apart: 7, of which 2 were waited for; matrix products, arithmetic and copies ran while one was open for 1% of the time, Pallas kernels for 35%

profile of v4, /device:TPU:11, one launch (start us, length us, event | category | flops | bytes accessed | tf_op | source)
XLA Modules:
  0.0 78.0 jit_solution(3942612483982667300)
XLA Ops:
  0.6 0.0 copy-start
  0.6 0.0 copy-start.3
  0.7 0.0 copy-start.4
  0.7 3.3 %pack.1 = (bf16[2,8,64,512]{3,2,1,0:T(8,128)(2,1)S(1)}, bf16[2,8,64,512]{3,2,1,0:T(8,128)(2,1)}, bf16[2,16,8,512]{3,2,1,0:T(8,128)(2,1)}) custom-call(f32[16,64,512]{2,1,0:T(8,128)} %bitcast.13, f32[16,64,512]{2,1,0:T(8,128)} %bitcast.22), custom_call_target="tpu_custom_call" | custom-call | tf_op jit(solution)/shard_map/pack/pallas_call | solution.py:51
  4.0 3.5 %collective-permute-start = (bf16[2,8,64,512]{3,2,1,0:T(8,128)(2,1)}, bf16[2,8,64,512]{3,2,1,0:T(8,128)(2,1)S(1)}, u32[]{:S(2)}, u32[]{:S(2)}) collective-permute-start(bf16[2,8,64,512]{3,2,1,0:T(8,128)(2,1)} %get-tuple-element.20), channel_id=1, source_target_pairs={{0,2},{1,3},{2,4},{3,5},{4,6},{5,7},{6,8},{7,9},{8,10},{9,11},{10,... | collective-permute-start | bytes 3145736 | tf_op jit(solution)/shard_map/ppermute | solution.py:486
  7.5 3.9 %collective-permute-start.1 = (bf16[2,8,64,512]{3,2,1,0:T(8,128)(2,1)S(1)}, bf16[2,8,64,512]{3,2,1,0:T(8,128)(2,1)S(1)}, u32[]{:S(2)}, u32[]{:S(2)}) collective-permute-start(bf16[2,8,64,512]{3,2,1,0:T(8,128)(2,1)S(1)} %get-tuple-element.21), channel_id=1, source_target_pairs={{2,0},{3,1},{4,2},{5,3},{6,4},{7,5},{8,6},{9,7},{10,8},{11,9},{12,... | collective-permute-start | bytes 3145736 | tf_op jit(solution)/shard_map/ppermute | solution.py:486
  11.5 2.4 %collective-permute-start.2 = (bf16[2,16,8,512]{3,2,1,0:T(8,128)(2,1)}, bf16[2,16,8,512]{3,2,1,0:T(8,128)(2,1)S(1)}, u32[]{:S(2)}, u32[]{:S(2)}) collective-permute-start(bf16[2,16,8,512]{3,2,1,0:T(8,128)(2,1)} %get-tuple-element.22), channel_id=1, source_target_pairs={{0,1},{1,0},{2,3},{3,2},{4,5},{5,4},{6,7},{7,6},{8,9},{9,8},{10,11... | collective-permute-start | bytes 786440 | tf_op jit(solution)/shard_map/ppermute | solution.py:486
  13.9 0.0 copy-done
  13.9 0.6 constant_dynamic-slice_fusion
  14.4 0.0 copy-done.3
  14.4 0.0 copy-done.4
  14.4 0.0 copy-start.2
  14.4 12.1 %network.1 = (bf16[1024,512]{1,0:T(8,128)(2,1)S(1)}, f32[1024,512]{1,0:T(8,128)S(1)}, f32[8,128]{1,0:T(8,128)S(1)}) custom-call(s32[1]{0:T(128)} %bitcast.1.count, s32[1,2048]{1,0:T(1,128)S(1)} %bitcast.19, f32[1,1024]{1,0:T(1,128)S(1)} %bitcast.21, f32[1024,512]{1,0:T(8,128)} %bitcast.14, bf16[1024,512]{1,0:T(8,128)(2,1)} %bitcast.29, ...), custom_call_target="tpu_custom_call" | custom-call | flops 7516192768 | bytes 12582912 | tf_op jit(solution)/shard_map/network/pallas_call | solution.py:416
  26.5 15.4 %collective-permute-done.2.strip = bf16[2,16,8,512]{3,2,1,0:T(8,128)(2,1)S(1)} collective-permute-done((bf16[2,16,8,512]{3,2,1,0:T(8,128)(2,1)}, bf16[2,16,8,512]{3,2,1,0:T(8,128)(2,1)S(1)}, u32[]{:S(2)}, u32[]{:S(2)}) %collective-permute-start.2) | collective-permute-done | bytes 262176 | tf_op jit(solution)/shard_map/ppermute | solution.py:486
  42.0 1.9 %collective-permute-start.3 = (bf16[2,6,8,512]{3,2,1,0:T(8,128)(2,1)S(1)}, bf16[2,6,8,512]{3,2,1,0:T(8,128)(2,1)S(1)}, u32[]{:S(2)}, u32[]{:S(2)}) collective-permute-start(bf16[2,6,8,512]{3,2,1,0:T(8,128)(2,1)S(1)} %get-tuple-element.24), channel_id=1, source_target_pairs={{0,2},{1,3},{2,4},{3,5},{4,6},{5,7},{6,8},{7,9},{8,10},{9,11},{10,... | collective-permute-start | bytes 294920 | tf_op jit(solution)/shard_map/ppermute | solution.py:486
  43.9 5.5 %collective-permute-start.4 = (bf16[2,6,8,512]{3,2,1,0:T(8,128)(2,1)S(1)}, bf16[2,6,8,512]{3,2,1,0:T(8,128)(2,1)S(1)}, u32[]{:S(2)}, u32[]{:S(2)}) collective-permute-start(bf16[2,6,8,512]{3,2,1,0:T(8,128)(2,1)S(1)} %get-tuple-element.25), channel_id=1, source_target_pairs={{2,0},{3,1},{4,2},{5,3},{6,4},{7,5},{8,6},{9,7},{10,8},{11,9},{12,... | collective-permute-start | bytes 294920 | tf_op jit(solution)/shard_map/ppermute | solution.py:486
  49.4 0.0 copy-done.2
  49.4 3.0 %inner.1 = (f32[4,32,88,128]{3,2,1,0:T(8,128)S(1)}, f32[4,32,88,128]{3,2,1,0:T(8,128)S(1)}) custom-call(f32[16,64,512]{2,1,0:T(8,128)} %bitcast.15, f32[16,64,512]{2,1,0:T(8,128)} %bitcast.24, bf16[2,16,8,512]{3,2,1,0:T(8,128)(2,1)S(1)} %collective-permute-done.2.strip, f32[8,512]{1,0:T(8,128)S(1)} %copy-done.2, f32[8,128]{1,0:T(8,128)S(1)} %get-tuple-element.26._), custom_call_target="tpu_custom_call" | custom-call | flops 14000000 | bytes 2097152 | tf_op jit(solution)/shard_map/inner/pallas_call | solution.py:296
  52.4 0.0 collective-permute-done.3.above_corner
  52.4 0.0 collective-permute-done.4.below_corner
  52.5 0.0 collective-permute-done.above
  52.5 0.0 collective-permute-done.1.below
  52.5 5.4 %outer.1 = (bf16[16,64,512]{2,1,0:T(8,128)(2,1)S(1)}, f32[4,32,88,128]{3,2,1,0:T(8,128)S(1)}, f32[4,32,88,128]{3,2,1,0:T(8,128)S(1)}) custom-call(bf16[2,8,64,512]{3,2,1,0:T(8,128)(2,1)S(1)} %collective-permute-done.above, bf16[2,8,64,512]{3,2,1,0:T(8,128)(2,1)S(1)} %collective-permute-done.1.below, ...), custom_call_target="tpu_custom_call", output_to_operand_aliasing={{1}: (5, {}), {2}: (6, {})} | custom-call | flops 36000000 | bytes 2097152 | tf_op jit(solution)/shard_map/outer/pallas_call | solution.py:310
  57.9 5.3 %collective-permute-start.5 = (bf16[16,64,512]{2,1,0:T(8,128)(2,1)S(1)}, bf16[16,64,512]{2,1,0:T(8,128)(2,1)S(1)}, u32[]{:S(2)}, u32[]{:S(2)}) collective-permute-start(bf16[16,64,512]{2,1,0:T(8,128)(2,1)S(1)} %get-tuple-element.29), channel_id=1, source_target_pairs={{16,32},{17,33},{18,34},{19,35},{20,36},{21,37},{22,38},{23,39},{2... | collective-permute-start | bytes 3145736 | tf_op jit(solution)/shard_map/ppermute | solution.py:486
  63.2 8.2 %staying.1 = (bf16[16,64,512]{2,1,0:T(8,128)(2,1)S(1)}, f32[8,128]{1,0:T(8,128)S(1)}) custom-call(f32[16,64,512]{2,1,0:T(8,128)} %bitcast.16, f32[16,64,512]{2,1,0:T(8,128)} %bitcast.25, bf16[2,8,64,512]{3,2,1,0:T(8,128)(2,1)S(1)} %collective-permute-done.above, bf16[2,8,64,512]{3,2,1,0:T(8,128)(2,1)S(1)} %collective-permute-done.1.below, ...), custom_call_target="tpu_custom_call" | custom-call | flops 50000000 | bytes 4194304 | tf_op jit(solution)/shard_map/staying/pallas_call | solution.py:277
  71.3 0.1 collective-permute-start.6
  71.4 0.0 copy-start.1
  71.5 4.0 %spread.1 = bf16[2048,512]{1,0:T(8,128)(2,1)} custom-call(s32[1]{0:T(128)} %bitcast.1.count, s32[1,2048]{1,0:T(1,128)S(1)} %bitcast.20, bf16[1024,512]{1,0:T(8,128)(2,1)S(1)} %get-tuple-element.33.tangents, f32[8,128]{1,0:T(8,128)S(1)} %get-tuple-element.34._), custom_call_target="tpu_custom_call" | custom-call | flops 2147483648 | bytes 4194304 | tf_op jit(solution)/shard_map/spread/pallas_call | solution.py:461
  75.5 0.2 collective-permute-done.5.from_chip
  75.7 0.0 collective-permute-done.6.from_core
  75.7 0.0 copy-done.1
  75.7 2.2 %final.1 = (f32[16,64,512]{2,1,0:T(8,128)}, f32[16,64,512]{2,1,0:T(8,128)}) custom-call(f32[16,64,512]{2,1,0:T(8,128)S(1)} %bitcast.17, f32[16,64,512]{2,1,0:T(8,128)S(1)} %bitcast.18, bf16[16,64,512]{2,1,0:T(8,128)(2,1)S(1)} %collective-permute-done.5.from_chip, bf16[16,64,512]{2,1,0:T(8,128)(2,1)S(1)} %collective-permute-done.6.from_core), custom_call_target="tpu_custom_call" | custom-call | flops 4000000 | bytes 10485760 | tf_op jit(solution)/shard_map/final/pallas_call | solution.py:345
  (1 shorter events, 0.0 us)
Async XLA Ops:
  0.6 13.2 %copy-start = (s32[1,16]{1,0:T(1,128)S(1)}, s32[1,16]{1,0:T(1,128)}, u32[]{:S(2)}) copy-start(s32[1,16]{1,0:T(1,128)} %param.15) | copy-start | bytes 196
  0.6 13.8 %copy-start.3 = (s32[1,1,2048]{2,1,0:T(1,128)S(1)}, s32[1,1,2048]{2,1,0:T(1,128)}, u32[]{:S(2)}) copy-start(s32[1,1,2048]{2,1,0:T(1,128)} %param.14) | copy-start | bytes 24580
  0.7 13.8 %copy-start.4 = (f32[1024]{0:T(1024)S(1)}, f32[1024]{0:T(1024)}, u32[]{:S(2)}) copy-start(f32[1024]{0:T(1024)} %param.18) | copy-start | bytes 12292
  4.0 48.5 %collective-permute-start = (bf16[2,8,64,512]{3,2,1,0:T(8,128)(2,1)}, bf16[2,8,64,512]{3,2,1,0:T(8,128)(2,1)S(1)}, u32[]{:S(2)}, u32[]{:S(2)}) collective-permute-start(bf16[2,8,64,512]{3,2,1,0:T(8,128)(2,1)} %get-tuple-element.20), channel_id=1, source_target_pairs={{0,2},{1,3},{2,4},{3,5},{4,6},{5,7},{6,8},{7,9},{8,10},{9,11},{10,... | collective-permute-start | bytes 3145736 | tf_op jit(solution)/shard_map/ppermute | solution.py:486
  7.5 44.9 %collective-permute-start.1 = (bf16[2,8,64,512]{3,2,1,0:T(8,128)(2,1)S(1)}, bf16[2,8,64,512]{3,2,1,0:T(8,128)(2,1)S(1)}, u32[]{:S(2)}, u32[]{:S(2)}) collective-permute-start(bf16[2,8,64,512]{3,2,1,0:T(8,128)(2,1)S(1)} %get-tuple-element.21), channel_id=1, source_target_pairs={{2,0},{3,1},{4,2},{5,3},{6,4},{7,5},{8,6},{9,7},{10,8},{11,9},{12,... | collective-permute-start | bytes 3145736 | tf_op jit(solution)/shard_map/ppermute | solution.py:486
  11.5 30.5 %collective-permute-start.2 = (bf16[2,16,8,512]{3,2,1,0:T(8,128)(2,1)}, bf16[2,16,8,512]{3,2,1,0:T(8,128)(2,1)S(1)}, u32[]{:S(2)}, u32[]{:S(2)}) collective-permute-start(bf16[2,16,8,512]{3,2,1,0:T(8,128)(2,1)} %get-tuple-element.22), channel_id=1, source_target_pairs={{0,1},{1,0},{2,3},{3,2},{4,5},{5,4},{6,7},{7,6},{8,9},{9,8},{10,11... | collective-permute-start | bytes 786440 | tf_op jit(solution)/shard_map/ppermute | solution.py:486
  14.4 34.9 %copy-start.2 = (f32[8,512]{1,0:T(8,128)S(1)}, f32[8,512]{1,0:T(8,128)}, u32[]{:S(2)}) copy-start(f32[8,512]{1,0:T(8,128)} %rates.5) | copy-start | bytes 49156
  42.0 10.5 %collective-permute-start.3 = (bf16[2,6,8,512]{3,2,1,0:T(8,128)(2,1)S(1)}, bf16[2,6,8,512]{3,2,1,0:T(8,128)(2,1)S(1)}, u32[]{:S(2)}, u32[]{:S(2)}) collective-permute-start(bf16[2,6,8,512]{3,2,1,0:T(8,128)(2,1)S(1)} %get-tuple-element.24), channel_id=1, source_target_pairs={{0,2},{1,3},{2,4},{3,5},{4,6},{5,7},{6,8},{7,9},{8,10},{9,11},{10,... | collective-permute-start | bytes 294920 | tf_op jit(solution)/shard_map/ppermute | solution.py:486
  43.9 8.5 %collective-permute-start.4 = (bf16[2,6,8,512]{3,2,1,0:T(8,128)(2,1)S(1)}, bf16[2,6,8,512]{3,2,1,0:T(8,128)(2,1)S(1)}, u32[]{:S(2)}, u32[]{:S(2)}) collective-permute-start(bf16[2,6,8,512]{3,2,1,0:T(8,128)(2,1)S(1)} %get-tuple-element.25), channel_id=1, source_target_pairs={{2,0},{3,1},{4,2},{5,3},{6,4},{7,5},{8,6},{9,7},{10,8},{11,9},{12,... | collective-permute-start | bytes 294920 | tf_op jit(solution)/shard_map/ppermute | solution.py:486
  57.9 17.8 %collective-permute-start.5 = (bf16[16,64,512]{2,1,0:T(8,128)(2,1)S(1)}, bf16[16,64,512]{2,1,0:T(8,128)(2,1)S(1)}, u32[]{:S(2)}, u32[]{:S(2)}) collective-permute-start(bf16[16,64,512]{2,1,0:T(8,128)(2,1)S(1)} %get-tuple-element.29), channel_id=1, source_target_pairs={{16,32},{17,33},{18,34},{19,35},{20,36},{21,37},{22,38},{23,39},{2... | collective-permute-start | bytes 3145736 | tf_op jit(solution)/shard_map/ppermute | solution.py:486
  71.3 4.3 %collective-permute-start.6 = (bf16[16,64,512]{2,1,0:T(8,128)(2,1)S(1)}, bf16[16,64,512]{2,1,0:T(8,128)(2,1)S(1)}, u32[]{:S(2)}, u32[]{:S(2)}) collective-permute-start(bf16[16,64,512]{2,1,0:T(8,128)(2,1)S(1)} %get-tuple-element.30), channel_id=1, source_target_pairs={{0,16},{1,17},{2,18},{3,19},{4,20},{5,21},{6,22},{7,23},{8,24},{9,... | collective-permute-start | bytes 3145736 | tf_op jit(solution)/shard_map/ppermute | solution.py:486
  71.4 4.3 %copy-start.1 = (f32[1,16,64,512]{3,2,1,0:T(8,128)S(1)}, f32[1,16,64,512]{3,2,1,0:T(8,128)}, u32[]{:S(2)}) copy-start(f32[1,16,64,512]{3,2,1,0:T(8,128)} %param.10) | copy-start | bytes 6291460

commit v5 on v4

--- a/solution.py
+++ b/solution.py
@@ -19,11 +19,15 @@
 CHUNK = 4
 
 
+def is_even_lat():
+    return lax.rem(lax.axis_index("lat"), 2) == 0
+
+
 def in_hbm(*arrays):
     return [pltpu.with_memory_space_constraint(a, pltpu.HBM) for a in arrays]
 
 
-def pack_kernel(inc, mul, low, high, strip, held, sems):
+def pack_kernel(inc, mul, near, far, strip, held, sems):
     lon = lax.axis_index("lon")
     rows, across = inc.shape[0], inc.shape[1]
     side = pl.multiple_of((across - REACH) * (1 - lon), REACH)
@@ -37,12 +41,18 @@
         for f in range(2):
             copies[f, start].wait()
             for r in range(start, start + CHUNK):
-                row = held[f, r].astype(jnp.bfloat16)
-                if r < REACH:
-                    low[f, r] = row
-                if r >= rows - REACH:
-                    high[f, r - rows + REACH] = row
                 strip[f, r] = held[f, r, pl.ds(side, REACH), :].astype(jnp.bfloat16)
+
+    even = is_even_lat()
+
+    def split(low, high):
+        for f in range(2):
+            for r in range(REACH):
+                low[f, r] = held[f, r].astype(jnp.bfloat16)
+                high[f, r] = held[f, rows - REACH + r].astype(jnp.bfloat16)
+
+    pl.when(even)(lambda: split(far, near))
+    pl.when(jnp.logical_not(even))(lambda: split(near, far))
 
 
 def pack(increment, multiplier):
@@ -62,10 +72,16 @@
     )(*in_hbm(increment, multiplier))
 
 
-def corner_kernel(strip, _, low, high, token):
+def corner_kernel(strip, _, near, far, token):
     rows = strip.shape[1]
-    low[...] = strip[:, :EDGE]
-    high[...] = strip[:, rows - EDGE :]
+    even = is_even_lat()
+
+    def split(low, high):
+        low[...] = strip[:, :EDGE]
+        high[...] = strip[:, rows - EDGE :]
+
+    pl.when(even)(lambda: split(far, near))
+    pl.when(jnp.logical_not(even))(lambda: split(near, far))
     token[...] = jnp.zeros_like(token)
 
 
@@ -145,21 +161,25 @@
     pltpu.make_async_copy(inc.at[:, :, pl.ds(0, LANES)], there, sems.at[t]).wait()
 
 
-def place_halo(forward, above, below, above_corner, below_corner, bufs):
-    tall, across = bufs.shape[1], above.shape[2]
+def place_halo(forward, near, far, near_corner, far_corner, bufs):
+    tall, across = bufs.shape[1], near.shape[2]
     rows = tall - 2 * REACH
     own, beside, _ = geometry(across)
     f = jnp.where(forward, 0, 1)
+    even = is_even_lat()
+    near_row, far_row = (jnp.where(e, rows + REACH, 0) for e in (even, jnp.logical_not(even)))
+    skip = REACH - EDGE
+    near_edge, far_edge = (jnp.where(e, rows + REACH, skip) for e in (even, jnp.logical_not(even)))
     for t in range(bufs.shape[0]):
         lanes = slice(t * LANES, (t + 1) * LANES)
         for r in (0, 1, tall - 2, tall - 1):
             bufs[t, r, pl.ds(beside, REACH), :] = jnp.zeros((REACH, LANES), jnp.float32)
         for r in range(REACH):
-            bufs[t, r, pl.ds(own, across), :] = above[f, r, :, lanes].astype(jnp.float32)
-            bufs[t, rows + REACH + r, pl.ds(own, across), :] = below[f, r, :, lanes].astype(jnp.float32)
+            bufs[t, near_row + r, pl.ds(own, across), :] = near[f, r, :, lanes].astype(jnp.float32)
+            bufs[t, far_row + r, pl.ds(own, across), :] = far[f, r, :, lanes].astype(jnp.float32)
         for r in range(EDGE):
-            bufs[t, REACH - EDGE + r, pl.ds(beside, REACH), :] = above_corner[f, r, :, lanes].astype(jnp.float32)
-            bufs[t, rows + REACH + r, pl.ds(beside, REACH), :] = below_corner[f, r, :, lanes].astype(jnp.float32)
+            bufs[t, near_edge + r, pl.ds(beside, REACH), :] = near_corner[f, r, :, lanes].astype(jnp.float32)
+            bufs[t, far_edge + r, pl.ds(beside, REACH), :] = far_corner[f, r, :, lanes].astype(jnp.float32)
 
 
 def taps_of(forward, rates, t):
@@ -204,14 +224,14 @@
         out[r, :, lanes] = (scale[0:1] * done[REACH + r, pl.ds(own, across), :]).astype(jnp.bfloat16)
 
 
-def whole_kernel(inc, mul, above, below, strip, above_corner, below_corner, rates, _, out, token, bufs, other, sems):
+def whole_kernel(inc, mul, near, far, strip, near_corner, far_corner, rates, _, out, token, bufs, other, sems):
     rows, across = inc.shape[0], inc.shape[1]
     blocks = (across + REACH) // 8
     tall = rows + 2 * REACH
     forward = is_forward(False)
     place_block(forward, inc, mul, strip, bufs, sems)
     token[...] = jnp.zeros_like(token)
-    place_halo(forward, above, below, above_corner, below_corner, bufs)
+    place_halo(forward, near, far, near_corner, far_corner, bufs)
     for r in range(tall):
         other[r] = jnp.zeros(other.shape[1:], jnp.float32)
     ranges = [[(2 * k, tall - 2 * k)] for k in range(1, STEPS + 1)]
@@ -246,12 +266,12 @@
     lax.fori_loop(0, bufs.shape[0], tile_of, 0)
 
 
-def outer_kernel(above, below, above_corner, below_corner, rates, _, __, out, bufs, other):
+def outer_kernel(near, far, near_corner, far_corner, rates, _, __, out, bufs, other):
     rows, across = out.shape[0], out.shape[1]
     blocks = (across + REACH) // 8
     tall = rows + 2 * REACH
     forward = is_forward(True)
-    place_halo(forward, above, below, above_corner, below_corner, bufs)
+    place_halo(forward, near, far, near_corner, far_corner, bufs)
     ranges = [
         [(2 * k, REACH + 2 * k), (REACH + rows - 2 * k, tall - 2 * k)] if k < STEPS else [(2 * k, tall - 2 * k)]
         for k in range(1, STEPS + 1)
@@ -306,7 +326,7 @@
 
 
 def crossing_outer(pieces, rates, bufs, other, shape):
-    above, below, _, above_corner, below_corner = pieces
+    near, far, _, near_corner, far_corner = pieces
     return pl.pallas_call(
         outer_kernel,
         in_specs=[VMEM] * 7,
@@ -320,7 +340,7 @@
         compiler_params=pltpu.CompilerParams(vmem_limit_bytes=20 << 20),
         cost_estimate=pl.CostEstimate(flops=36_000_000, bytes_accessed=2 << 20, transcendentals=0),
         name="outer",
-    )(above, below, above_corner, below_corner, rates, bufs, other)[0]
+    )(near, far, near_corner, far_corner, rates, bufs, other)[0]
 
 
 def final_kernel(inc, base, from_chip, from_core, error_out, grad_out, error, grad, sems):
@@ -500,9 +520,11 @@
 ):
     increment, multiplier = increment[0], multiplier[0]
     levels = increment.shape[2]
-    low, high, strip = pack(increment, multiplier)
-    above = sent(high, lambda s, a, o: (s, a + 1, o))
-    below = sent(low, lambda s, a, o: (s, a - 1, o))
+    near_out, far_out, strip = pack(increment, multiplier)
+    partner = lambda s, a, o: (s, a - 1 if a % 2 else a + 1, o)
+    other_side = lambda s, a, o: (s, a + 1 if a % 2 else a - 1, o)
+    near = sent(near_out, partner)
+    far = sent(far_out, other_side)
     across = sent(strip, lambda s, a, o: (s, a, 1 - o))
     myself = lax.axis_index(("lat", "lon"))
     my_count = lax.dynamic_slice(obs_count[0], (myself,), (1,))
@@ -517,11 +539,10 @@
         hidden_bias[None, :],
         output_weight,
     )
-    low_corner, high_corner, token = corners(across, token)
-    above_corner = sent(high_corner, lambda s, a, o: (s, a + 1, o))
-    below_corner = sent(low_corner, lambda s, a, o: (s, a - 1, o))
-    pieces = [above, below, across, above_corner, below_corner]
-    pieces = [above, below, across, above_corner, below_corner]
+    near_corner, far_corner, token = corners(across, token)
+    near_corner = sent(near_corner, partner)
+    far_corner = sent(far_corner, other_side)
+    pieces = [near, far, across, near_corner, far_corner]
     bufs, other = crossing_inner(increment, multiplier, across, transport, token)
     crossing = crossing_outer(pieces, transport, bufs, other, increment.shape)
     from_chip = sent(crossing, lambda s, a, o: (s + 1 if s % 2 else s - 1, a, o))

time: 78.4 us -> 74.5 us (0.950)
  starting transfers between devices: 22.6 us -> 18.1 us
    ppermute x7, starting transfers between devices: 22.6 us -> 18.1 us  [sent(): return lax.ppermute(array, ('sub', 'lat', 'lon'), pairs)]
  transfers between devices with their start and end apart: 7 -> 7, of which waited for: 2 -> 3; matrix products, arithmetic and copies ran while one was open for 1% -> 1% of each run, Pallas kernels for 35% -> 37%
where the time goes in v5:
time: 74.5 us; the launch traced here: 74.2 us
  Pallas kernels  38.4 us (52%)
  starting transfers between devices  18.1 us (24%)
  waiting for transfers between devices  16.1 us (22%)
  between operations  0.94 us (1%)
    ppermute x7, starting transfers between devices, sent(): return lax.ppermute(array, ('sub', 'lat', 'lon'), pairs)  18.1 us
    ppermute x7, waiting for transfers between devices, sent(): return lax.ppermute(array, ('sub', 'lat', 'lon'), pairs)  16.1 us
    pallas_call x1, Pallas kernels, network(): pl.pallas_call(network_kernel, in_specs=[pl.BlockSpec(memory_space=pltpu....  12.1 us
    pallas_call x1, Pallas kernels, staying_field(): pl.pallas_call(whole_kernel, in_specs=[HBM, HBM] + [VMEM] * (len(pieces)...  8.18 us
    pallas_call x1, Pallas kernels, crossing_outer(): pl.pallas_call(outer_kernel, in_specs=[VMEM] * 7, out_specs=[VMEM] * 3, o...  5.46 us
    pallas_call x1, Pallas kernels, spread(): pl.pallas_call(spread_kernel, in_specs=[pl.BlockSpec(memory_space=pltpu.S...  4.02 us
    pallas_call x1, Pallas kernels, pack(): pl.pallas_call(pack_kernel, in_specs=[pl.BlockSpec(memory_space=pltpu.HBM...  3.49 us
    pallas_call x1, Pallas kernels, crossing_inner(): pl.pallas_call(inner_kernel, in_specs=[HBM, HBM, VMEM, VMEM, ANY], out_sp...  3.03 us
  transfers between devices with their start and end apart: 7, of which 3 were waited for; matrix products, arithmetic and copies ran while one was open for 1% of the time, Pallas kernels for 37%

profile of v5, /device:TPU:11, one launch (start us, length us, event | category | flops | bytes accessed | tf_op | source)
XLA Modules:
  0.0 74.2 jit_solution(4538637093005118795)
XLA Ops:
  0.6 0.0 copy-start
  0.6 0.0 copy-start.3
  0.7 0.0 copy-start.4
  0.7 3.5 %pack.1 = (bf16[2,8,64,512]{3,2,1,0:T(8,128)(2,1)}, bf16[2,8,64,512]{3,2,1,0:T(8,128)(2,1)S(1)}, bf16[2,16,8,512]{3,2,1,0:T(8,128)(2,1)}) custom-call(f32[16,64,512]{2,1,0:T(8,128)} %bitcast.13, f32[16,64,512]{2,1,0:T(8,128)} %bitcast.22), custom_call_target="tpu_custom_call" | custom-call | tf_op jit(solution)/shard_map/pack/pallas_call | solution.py:61
  4.2 1.7 %collective-permute-start = (bf16[2,8,64,512]{3,2,1,0:T(8,128)(2,1)}, bf16[2,8,64,512]{3,2,1,0:T(8,128)(2,1)S(1)}, u32[]{:S(2)}, u32[]{:S(2)}) collective-permute-start(bf16[2,8,64,512]{3,2,1,0:T(8,128)(2,1)} %get-tuple-element.20), channel_id=1, source_target_pairs={{0,2},{1,3},{2,0},{3,1},{4,6},{5,7},{6,4},{7,5},{8,10},{9,11},{10,... | collective-permute-start | bytes 3145736 | tf_op jit(solution)/shard_map/ppermute | solution.py:506
  5.9 4.0 %collective-permute-start.1 = (bf16[2,8,64,512]{3,2,1,0:T(8,128)(2,1)S(1)}, bf16[2,8,64,512]{3,2,1,0:T(8,128)(2,1)S(1)}, u32[]{:S(2)}, u32[]{:S(2)}) collective-permute-start(bf16[2,8,64,512]{3,2,1,0:T(8,128)(2,1)S(1)} %get-tuple-element.21), channel_id=1, source_target_pairs={{2,4},{3,5},{4,2},{5,3},{6,8},{7,9},{8,6},{9,7},{10,12},{11,13},{1... | collective-permute-start | bytes 3145736 | tf_op jit(solution)/shard_map/ppermute | solution.py:506
  9.9 2.4 %collective-permute-start.2 = (bf16[2,16,8,512]{3,2,1,0:T(8,128)(2,1)}, bf16[2,16,8,512]{3,2,1,0:T(8,128)(2,1)S(1)}, u32[]{:S(2)}, u32[]{:S(2)}) collective-permute-start(bf16[2,16,8,512]{3,2,1,0:T(8,128)(2,1)} %get-tuple-element.22), channel_id=1, source_target_pairs={{0,1},{1,0},{2,3},{3,2},{4,5},{5,4},{6,7},{7,6},{8,9},{9,8},{10,11... | collective-permute-start | bytes 786440 | tf_op jit(solution)/shard_map/ppermute | solution.py:506
  12.3 0.0 copy-done
  12.3 0.6 constant_dynamic-slice_fusion
  12.9 0.0 copy-done.3
  12.9 0.0 copy-done.4
  12.9 0.0 copy-start.2
  12.9 12.1 %network.1 = (bf16[1024,512]{1,0:T(8,128)(2,1)S(1)}, f32[1024,512]{1,0:T(8,128)S(1)}, f32[8,128]{1,0:T(8,128)S(1)}) custom-call(s32[1]{0:T(128)} %bitcast.1.count, s32[1,2048]{1,0:T(1,128)S(1)} %bitcast.19, f32[1,1024]{1,0:T(1,128)S(1)} %bitcast.21, f32[1024,512]{1,0:T(8,128)} %bitcast.14, bf16[1024,512]{1,0:T(8,128)(2,1)} %bitcast.29, ...), custom_call_target="tpu_custom_call" | custom-call | flops 7516192768 | bytes 12582912 | tf_op jit(solution)/shard_map/network/pallas_call | solution.py:436
  25.0 15.1 %collective-permute-done.2.strip = bf16[2,16,8,512]{3,2,1,0:T(8,128)(2,1)S(1)} collective-permute-done((bf16[2,16,8,512]{3,2,1,0:T(8,128)(2,1)}, bf16[2,16,8,512]{3,2,1,0:T(8,128)(2,1)S(1)}, u32[]{:S(2)}, u32[]{:S(2)}) %collective-permute-start.2) | collective-permute-done | bytes 262176 | tf_op jit(solution)/shard_map/ppermute | solution.py:506
  40.1 0.1 collective-permute-start.3
  40.2 3.7 %collective-permute-start.4 = (bf16[2,6,8,512]{3,2,1,0:T(8,128)(2,1)S(1)}, bf16[2,6,8,512]{3,2,1,0:T(8,128)(2,1)S(1)}, u32[]{:S(2)}, u32[]{:S(2)}) collective-permute-start(bf16[2,6,8,512]{3,2,1,0:T(8,128)(2,1)S(1)} %get-tuple-element.25), channel_id=1, source_target_pairs={{2,4},{3,5},{4,2},{5,3},{6,8},{7,9},{8,6},{9,7},{10,12},{11,13},{1... | collective-permute-start | bytes 294920 | tf_op jit(solution)/shard_map/ppermute | solution.py:506
  43.9 0.0 copy-done.2
  43.9 3.0 %inner.1 = (f32[4,32,88,128]{3,2,1,0:T(8,128)S(1)}, f32[4,32,88,128]{3,2,1,0:T(8,128)S(1)}) custom-call(f32[16,64,512]{2,1,0:T(8,128)} %bitcast.15, f32[16,64,512]{2,1,0:T(8,128)} %bitcast.24, bf16[2,16,8,512]{3,2,1,0:T(8,128)(2,1)S(1)} %collective-permute-done.2.strip, f32[8,512]{1,0:T(8,128)S(1)} %copy-done.2, f32[8,128]{1,0:T(8,128)S(1)} %get-tuple-element.26._), custom_call_target="tpu_custom_call" | custom-call | flops 14000000 | bytes 2097152 | tf_op jit(solution)/shard_map/inner/pallas_call | solution.py:316
  47.0 0.0 collective-permute-done.3.near_corner
  47.0 0.7 collective-permute-done.4.far_corner
  47.7 0.0 collective-permute-done.near
  47.7 0.0 collective-permute-done.1.far
  47.7 5.5 %outer.1 = (bf16[16,64,512]{2,1,0:T(8,128)(2,1)S(1)}, f32[4,32,88,128]{3,2,1,0:T(8,128)S(1)}, f32[4,32,88,128]{3,2,1,0:T(8,128)S(1)}) custom-call(bf16[2,8,64,512]{3,2,1,0:T(8,128)(2,1)S(1)} %collective-permute-done.near, bf16[2,8,64,512]{3,2,1,0:T(8,128)(2,1)S(1)} %collective-permute-done.1.far, ...), custom_call_target="tpu_custom_call", output_to_operand_aliasing={{1}: (5, {}), {2}: (6, {})} | custom-call | flops 36000000 | bytes 2097152 | tf_op jit(solution)/shard_map/outer/pallas_call | solution.py:330
  53.2 6.1 %collective-permute-start.5 = (bf16[16,64,512]{2,1,0:T(8,128)(2,1)S(1)}, bf16[16,64,512]{2,1,0:T(8,128)(2,1)S(1)}, u32[]{:S(2)}, u32[]{:S(2)}) collective-permute-start(bf16[16,64,512]{2,1,0:T(8,128)(2,1)S(1)} %get-tuple-element.29), channel_id=1, source_target_pairs={{16,32},{17,33},{18,34},{19,35},{20,36},{21,37},{22,38},{23,39},{2... | collective-permute-start | bytes 3145736 | tf_op jit(solution)/shard_map/ppermute | solution.py:506
  59.3 8.2 %staying.1 = (bf16[16,64,512]{2,1,0:T(8,128)(2,1)S(1)}, f32[8,128]{1,0:T(8,128)S(1)}) custom-call(f32[16,64,512]{2,1,0:T(8,128)} %bitcast.16, f32[16,64,512]{2,1,0:T(8,128)} %bitcast.25, bf16[2,8,64,512]{3,2,1,0:T(8,128)(2,1)S(1)} %collective-permute-done.near, bf16[2,8,64,512]{3,2,1,0:T(8,128)(2,1)S(1)} %collective-permute-done.1.far, ...), custom_call_target="tpu_custom_call" | custom-call | flops 50000000 | bytes 4194304 | tf_op jit(solution)/shard_map/staying/pallas_call | solution.py:297
  67.5 0.1 collective-permute-start.6
  67.6 0.0 copy-start.1
  67.6 4.0 %spread.1 = bf16[2048,512]{1,0:T(8,128)(2,1)} custom-call(s32[1]{0:T(128)} %bitcast.1.count, s32[1,2048]{1,0:T(1,128)S(1)} %bitcast.20, bf16[1024,512]{1,0:T(8,128)(2,1)S(1)} %get-tuple-element.33.tangents, f32[8,128]{1,0:T(8,128)S(1)} %get-tuple-element.34._), custom_call_target="tpu_custom_call" | custom-call | flops 2147483648 | bytes 4194304 | tf_op jit(solution)/shard_map/spread/pallas_call | solution.py:481
  71.6 0.2 collective-permute-done.5.from_chip
  71.9 0.0 collective-permute-done.6.from_core
  71.9 0.0 copy-done.1
  71.9 2.2 %final.1 = (f32[16,64,512]{2,1,0:T(8,128)}, f32[16,64,512]{2,1,0:T(8,128)}) custom-call(f32[16,64,512]{2,1,0:T(8,128)S(1)} %bitcast.17, f32[16,64,512]{2,1,0:T(8,128)S(1)} %bitcast.18, bf16[16,64,512]{2,1,0:T(8,128)(2,1)S(1)} %collective-permute-done.5.from_chip, bf16[16,64,512]{2,1,0:T(8,128)(2,1)S(1)} %collective-permute-done.6.from_core), custom_call_target="tpu_custom_call" | custom-call | flops 4000000 | bytes 10485760 | tf_op jit(solution)/shard_map/final/pallas_call | solution.py:365
  (1 shorter events, 0.0 us)
Async XLA Ops:
  0.6 11.7 %copy-start = (s32[1,16]{1,0:T(1,128)S(1)}, s32[1,16]{1,0:T(1,128)}, u32[]{:S(2)}) copy-start(s32[1,16]{1,0:T(1,128)} %param.15) | copy-start | bytes 196
  0.6 12.2 %copy-start.3 = (s32[1,1,2048]{2,1,0:T(1,128)S(1)}, s32[1,1,2048]{2,1,0:T(1,128)}, u32[]{:S(2)}) copy-start(s32[1,1,2048]{2,1,0:T(1,128)} %param.14) | copy-start | bytes 24580
  0.7 12.2 %copy-start.4 = (f32[1024]{0:T(1024)S(1)}, f32[1024]{0:T(1024)}, u32[]{:S(2)}) copy-start(f32[1024]{0:T(1024)} %param.18) | copy-start | bytes 12292
  4.2 43.5 %collective-permute-start = (bf16[2,8,64,512]{3,2,1,0:T(8,128)(2,1)}, bf16[2,8,64,512]{3,2,1,0:T(8,128)(2,1)S(1)}, u32[]{:S(2)}, u32[]{:S(2)}) collective-permute-start(bf16[2,8,64,512]{3,2,1,0:T(8,128)(2,1)} %get-tuple-element.20), channel_id=1, source_target_pairs={{0,2},{1,3},{2,0},{3,1},{4,6},{5,7},{6,4},{7,5},{8,10},{9,11},{10,... | collective-permute-start | bytes 3145736 | tf_op jit(solution)/shard_map/ppermute | solution.py:506
  5.9 41.8 %collective-permute-start.1 = (bf16[2,8,64,512]{3,2,1,0:T(8,128)(2,1)S(1)}, bf16[2,8,64,512]{3,2,1,0:T(8,128)(2,1)S(1)}, u32[]{:S(2)}, u32[]{:S(2)}) collective-permute-start(bf16[2,8,64,512]{3,2,1,0:T(8,128)(2,1)S(1)} %get-tuple-element.21), channel_id=1, source_target_pairs={{2,4},{3,5},{4,2},{5,3},{6,8},{7,9},{8,6},{9,7},{10,12},{11,13},{1... | collective-permute-start | bytes 3145736 | tf_op jit(solution)/shard_map/ppermute | solution.py:506
  9.9 30.2 %collective-permute-start.2 = (bf16[2,16,8,512]{3,2,1,0:T(8,128)(2,1)}, bf16[2,16,8,512]{3,2,1,0:T(8,128)(2,1)S(1)}, u32[]{:S(2)}, u32[]{:S(2)}) collective-permute-start(bf16[2,16,8,512]{3,2,1,0:T(8,128)(2,1)} %get-tuple-element.22), channel_id=1, source_target_pairs={{0,1},{1,0},{2,3},{3,2},{4,5},{5,4},{6,7},{7,6},{8,9},{9,8},{10,11... | collective-permute-start | bytes 786440 | tf_op jit(solution)/shard_map/ppermute | solution.py:506
  12.9 31.0 %copy-start.2 = (f32[8,512]{1,0:T(8,128)S(1)}, f32[8,512]{1,0:T(8,128)}, u32[]{:S(2)}) copy-start(f32[8,512]{1,0:T(8,128)} %rates.5) | copy-start | bytes 49156
  40.1 6.8 %collective-permute-start.3 = (bf16[2,6,8,512]{3,2,1,0:T(8,128)(2,1)S(1)}, bf16[2,6,8,512]{3,2,1,0:T(8,128)(2,1)S(1)}, u32[]{:S(2)}, u32[]{:S(2)}) collective-permute-start(bf16[2,6,8,512]{3,2,1,0:T(8,128)(2,1)S(1)} %get-tuple-element.24), channel_id=1, source_target_pairs={{0,2},{1,3},{2,0},{3,1},{4,6},{5,7},{6,4},{7,5},{8,10},{9,11},{10,... | collective-permute-start | bytes 294920 | tf_op jit(solution)/shard_map/ppermute | solution.py:506
  40.2 7.5 %collective-permute-start.4 = (bf16[2,6,8,512]{3,2,1,0:T(8,128)(2,1)S(1)}, bf16[2,6,8,512]{3,2,1,0:T(8,128)(2,1)S(1)}, u32[]{:S(2)}, u32[]{:S(2)}) collective-permute-start(bf16[2,6,8,512]{3,2,1,0:T(8,128)(2,1)S(1)} %get-tuple-element.25), channel_id=1, source_target_pairs={{2,4},{3,5},{4,2},{5,3},{6,8},{7,9},{8,6},{9,7},{10,12},{11,13},{1... | collective-permute-start | bytes 294920 | tf_op jit(solution)/shard_map/ppermute | solution.py:506
  53.2 18.7 %collective-permute-start.5 = (bf16[16,64,512]{2,1,0:T(8,128)(2,1)S(1)}, bf16[16,64,512]{2,1,0:T(8,128)(2,1)S(1)}, u32[]{:S(2)}, u32[]{:S(2)}) collective-permute-start(bf16[16,64,512]{2,1,0:T(8,128)(2,1)S(1)} %get-tuple-element.29), channel_id=1, source_target_pairs={{16,32},{17,33},{18,34},{19,35},{20,36},{21,37},{22,38},{23,39},{2... | collective-permute-start | bytes 3145736 | tf_op jit(solution)/shard_map/ppermute | solution.py:506
  67.5 4.3 %collective-permute-start.6 = (bf16[16,64,512]{2,1,0:T(8,128)(2,1)S(1)}, bf16[16,64,512]{2,1,0:T(8,128)(2,1)S(1)}, u32[]{:S(2)}, u32[]{:S(2)}) collective-permute-start(bf16[16,64,512]{2,1,0:T(8,128)(2,1)S(1)} %get-tuple-element.30), channel_id=1, source_target_pairs={{0,16},{1,17},{2,18},{3,19},{4,20},{5,21},{6,22},{7,23},{8,24},{9,... | collective-permute-start | bytes 3145736 | tf_op jit(solution)/shard_map/ppermute | solution.py:506
  67.6 4.3 %copy-start.1 = (f32[1,16,64,512]{3,2,1,0:T(8,128)S(1)}, f32[1,16,64,512]{3,2,1,0:T(8,128)}, u32[]{:S(2)}) copy-start(f32[1,16,64,512]{3,2,1,0:T(8,128)} %param.10) | copy-start | bytes 6291460
